TPU v7x, 32 devices: a whole 2x2x4 slice. The times are simulated.
32 devices in a mesh: blk: 16 (over z, y, core), head: 2 (over x).
Axes of the slice: x: 2, y: 2, z: 4, core: 2. Of those that a mesh axis runs over, the one named last changes fastest.
Arguments:
- queries: bfloat16 [4096, 1024], P('blk', 'head'), may hold values from -216 to 216
- keys: bfloat16 [4096, 1024], P('blk', 'head'), may hold values from -6 to 6
- values: bfloat16 [4096, 1024], P('blk', 'head'), may hold values from -6 to 6
- group_table: int32 [16, 2], P('blk'), may hold values from 0 to 31, as said below
- doc_ids: int32 [4096], replicated, may hold values from 0 to 15, never falling along the last dimension, each value on 1 to 2048 neighbouring positions
Outputs:
- attended: bfloat16 [4096, 1024], P('blk', 'head')
Inputs may be any that keep to these rules, and one draw needn't show every extreme that they name: group_table[d, 1] = 31 - group_table[d, 0]; the first column holds each of 0 to 15 once. `doc_ids`: document numbers never fall along positions; a document holds at most 2048 positions.
All inputs are finite; a program needn't handle non-finite values.
Results may differ from a plain program's by a relative error of at most 0.0049.
Values may be sent and summed in bfloat16 or wider, within the bound.
No kernel may reach another device: no remote copies, remote signals or barrier semaphores. Data moves between devices by JAX's collectives and lax.ppermute only.
A program may use at most 192 MiB of HBM per device.

v0:
```python
import math

import jax
import jax.numpy as jnp
from jax import lax
from jax.sharding import PartitionSpec as P

HEAD_DIM = 128


def shards(queries, keys, values, group_table, doc_ids):
    tok_rows = queries.shape[0]
    group_rows = tok_rows // 2
    head_count = queries.shape[1] // HEAD_DIM
    score_scale = 1.0 / math.sqrt(HEAD_DIM)
    whole_table = lax.all_gather(group_table, "blk", axis=0, tiled=True)
    group_docs = doc_ids.reshape(doc_ids.shape[0] // group_rows, group_rows)
    within = jnp.arange(group_rows, dtype=jnp.int32)
    stored_groups = whole_table.reshape(-1)
    all_key_pos = (stored_groups[:, None] * group_rows + within[None, :]).reshape(-1)
    all_key_doc = group_docs[stored_groups].reshape(-1)
    local_groups = group_table.reshape(-1)
    query_pos = (local_groups[:, None] * group_rows + within[None, :]).reshape(-1)
    query_doc = group_docs[local_groups].reshape(-1)
    query_heads = queries.reshape(tok_rows, head_count, HEAD_DIM)

    def attend_shard(running_state, key_piece, value_piece, offset):
        piece_rows = key_piece.shape[0]
        key_pos = lax.dynamic_slice_in_dim(all_key_pos, offset, piece_rows, 0)
        key_doc = lax.dynamic_slice_in_dim(all_key_doc, offset, piece_rows, 0)
        visible = (query_doc[:, None] == key_doc[None, :]) & (
            key_pos[None, :] <= query_pos[:, None]
        )
        summed, running_max, weight_sum = running_state
        key_heads = key_piece.reshape(piece_rows, head_count, HEAD_DIM)
        value_heads = value_piece.reshape(piece_rows, head_count, HEAD_DIM)
        scores = (
            jnp.einsum("qhd,khd->hqk", query_heads, key_heads, preferred_element_type=jnp.float32)
            * score_scale
        )
        scores = jnp.where(visible[None], scores, -1e30)
        new_max = jnp.maximum(running_max, jnp.max(scores, axis=-1))
        weights = jnp.where(visible[None], jnp.exp(scores - new_max[..., None]), 0.0)
        factor = jnp.exp(running_max - new_max)
        weight_sum = weight_sum * factor + jnp.sum(weights, axis=-1)
        summed = summed * jnp.transpose(factor)[..., None] + jnp.einsum(
            "hqk,khd->qhd",
            weights.astype(jnp.bfloat16),
            value_heads,
            preferred_element_type=jnp.float32,
        )
        return (summed, new_max, weight_sum)

    initial = (
        jnp.zeros((tok_rows, head_count, HEAD_DIM), jnp.float32),
        jnp.full((head_count, tok_rows), -1e30, jnp.float32),
        jnp.zeros((head_count, tok_rows), jnp.float32),
    )
    key_piece = lax.all_gather(keys, "blk", axis=0, tiled=True)
    value_piece = lax.all_gather(values, "blk", axis=0, tiled=True)
    shard_count = key_piece.shape[0] // tok_rows
    key_shards = key_piece.reshape(shard_count, tok_rows, key_piece.shape[1])
    value_shards = value_piece.reshape(shard_count, tok_rows, value_piece.shape[1])
    shard_ids = jnp.arange(shard_count, dtype=jnp.int32)

    def step(state_now, item):
        key_one, value_one, shard_index = item
        start = shard_index * tok_rows
        return (attend_shard(state_now, key_one, value_one, start), None)

    final_state, unused = lax.scan(step, initial, (key_shards, value_shards, shard_ids))
    summed, running_max, weight_sum = final_state
    output = summed / jnp.transpose(weight_sum)[..., None]
    return output.reshape(tok_rows, head_count * HEAD_DIM).astype(jnp.bfloat16)


def solution(mesh):
    in_specs = (P("blk", "head"), P("blk", "head"), P("blk", "head"), P("blk", None), P())
    out_specs = P("blk", "head")
    return jax.shard_map(shards, mesh=mesh, in_specs=in_specs, out_specs=out_specs, check_vma=False)
```

profile of v0, /device:TPU:0, one launch (start us, length us, event | category | flops | bytes accessed | tf_op | source)
XLA Modules:
  0.0 186.2 jit_solution(14628548293793121357)
XLA Ops:
  6.5 0.7 all-gather.4.cloned.1.call-update
  7.3 0.7 all-gather.6.cloned.1.call-update
  8.0 23.3 %all-gather = s32[16,1,2]{2,1,0:T(1,128)S(1)} all-gather(s32[1,1,2]{2,1,0:T(1,128)} %bitcast.68), channel_id=1, replica_groups=mesh['blk'=16,'head'=2] {'blk'}, dimensions={0}, use_global_device_ids=true | all-gather | bytes 136 | tf_op jit(solution)/shard_map/all_gather | solution.py:16
  31.4 0.5 broadcast.150
  31.9 0.7 multiply_reduce_fusion
  32.8 0.6 gather_fusion.1
  33.3 0.7 fusion.14
  34.0 0.6 gather_fusion
  34.6 1.1 copy.23
  35.8 0.7 multiply_bitcast_fusion
  36.6 26.1 %all-gather.4.cloned.1.call-done = bf16[4096,512]{1,0:T(8,128)(2,1)} async-done(((bf16[256,512]{1,0:T(8,128)(2,1)}), bf16[4096,512]{1,0:T(8,128)(2,1)}) %all-gather.4.cloned.1.call-update) | async-done | bytes 4194320 | tf_op jit(solution)/shard_map/all_gather | solution.py:59
  62.7 51.1 %all-gather.6.cloned.1.call-done = bf16[4096,512]{1,0:T(8,128)(2,1)} async-done(((bf16[256,512]{1,0:T(8,128)(2,1)}), bf16[4096,512]{1,0:T(8,128)(2,1)}) %all-gather.6.cloned.1.call-update) | async-done | bytes 4194320 | tf_op jit(solution)/shard_map/all_gather | solution.py:60
  113.8 64.7 %while.15 = (s32[]{:T(128)}, f32[256,4,128]{0,2,1:T(8,128)S(1)}, f32[4,256]{1,0:T(4,128)S(1)}, f32[4,256]{1,0:T(4,128)S(1)}, s32[2,128]{1,0:T(2,128)S(1)}, /*ind...) while((s32[]{:T(128)}, f32[256,4,128]{0,2,1:T(8,128)S(1)}, ...), condition=%wide.region_3.4_spmd.clone, body=%wide.region_0.3_spmd.clone.sunk | while | flops 137173248 | bytes 7415023 | solution.py:71
  113.8 0.6 dynamic_slice.29
  115.4 1.1 constant_dynamic-slice_fusion.3
  117.8 0.6 dynamic_slice.29
  119.4 1.1 constant_dynamic-slice_fusion.3
  121.9 0.6 dynamic_slice.29
  123.5 1.1 constant_dynamic-slice_fusion.3
  125.9 0.6 dynamic_slice.29
  127.5 1.1 constant_dynamic-slice_fusion.3
  129.5 0.4 fusion.35
  129.9 0.6 dynamic_slice.29
  131.5 1.1 constant_dynamic-slice_fusion.3
  133.5 0.4 fusion.35
  134.0 0.6 dynamic_slice.29
  135.6 1.1 constant_dynamic-slice_fusion.3
  138.0 0.6 dynamic_slice.29
  139.6 1.1 constant_dynamic-slice_fusion.3
  142.1 0.6 dynamic_slice.29
  143.7 1.1 constant_dynamic-slice_fusion.3
  146.1 0.6 dynamic_slice.29
  147.7 1.1 constant_dynamic-slice_fusion.3
  150.2 0.6 dynamic_slice.29
  151.8 1.1 constant_dynamic-slice_fusion.3
  154.2 0.6 dynamic_slice.29
  155.8 1.1 constant_dynamic-slice_fusion.3
  158.2 0.6 dynamic_slice.29
  159.8 1.1 constant_dynamic-slice_fusion.3
  162.3 0.6 dynamic_slice.29
  163.9 1.1 constant_dynamic-slice_fusion.3
  166.3 0.6 dynamic_slice.29
  167.9 1.1 constant_dynamic-slice_fusion.3
  170.4 0.6 dynamic_slice.29
  172.0 1.1 constant_dynamic-slice_fusion.3
  174.4 0.6 dynamic_slice.29
  176.0 1.1 constant_dynamic-slice_fusion.3
  178.5 0.8 copy.30
  (206 shorter events, 26.2 us)
Async XLA Ops:
  6.5 26.2 %copy-start = (s32[4096]{0:T(1024)S(1)}, s32[4096]{0:T(1024)}, u32[]{:S(2)}) copy-start(s32[4096]{0:T(1024)} %param.11) | copy-start | bytes 49156
  6.5 56.1 %all-gather.4.cloned.1.call-start = ((), (), s32[]{:S(2)}) async-start(), calls=%async_computation | async-start | bytes 4456448 | tf_op jit(solution)/shard_map/all_gather | solution.py:59
  7.3 106.5 %all-gather.6.cloned.1.call-start = ((), (), s32[]{:S(2)}) async-start(), calls=%async_computation.1 | async-start | bytes 4456448 | tf_op jit(solution)/shard_map/all_gather | solution.py:60
Sparse Core Ops, SparseCore 0:
  9.5 53.1 all-gather.3
  64.8 48.8 all-gather.5
where the time goes:
time: 187 us; the launch traced here: 186 us
  waiting for transfers between devices  78.6 us (42%)
  local copies, waits for them, and re-layouts  37.4 us (20%)
  blocking collectives  23.3 us (12%)
  between operations  13.5 us (7%)
  matrix products  12.7 us (7%)
  loops' own time  11.4 us (6%)
  other arithmetic  9.23 us (5%)
    all_gather x1, waiting for transfers between devices, shards(): value_piece = lax.all_gather(values, 'blk', axis=0, tiled=True)  51.1 us
    dynamic_slice x64, local copies, waits for them, and re-layouts, shards(): lax.scan(step, initial, (key_shards, value_shards, shard_ids))  31 us
    all_gather x1, waiting for transfers between devices, shards(): key_piece = lax.all_gather(keys, 'blk', axis=0, tiled=True)  26.1 us
    all_gather x1, blocking collectives, shards(): whole_table = lax.all_gather(group_table, 'blk', axis=0, tiled=True)  23.3 us
    another operation x1, loops' own time, shards(): lax.scan(step, initial, (key_shards, value_shards, shard_ids))  11.4 us
    dot_general x16, matrix products, attend_shard(): jnp.einsum('hqk,khd->qhd', weights.astype(jnp.bfloat16), value_heads, pre...  6.68 us
    dot_general x16, matrix products, attend_shard(): jnp.einsum('qhd,khd->hqk', query_heads, key_heads, preferred_element_type...  6.02 us
  transfers between devices with their start and end apart: 2, of which 2 were waited for; matrix products, arithmetic and copies ran while one was open for 3% of the time, Pallas kernels for 0%

commit v1 on v0

v1 whole, which is shorter than its diff:
```python
import functools
import math

import jax
import jax.numpy as jnp
from jax import lax
from jax.experimental import pallas as pl
from jax.experimental.pallas import tpu as pltpu
from jax.sharding import PartitionSpec as P

HEAD_DIM = 128
CHUNK = 512
HIDDEN = -1e30


def attend_kernel(n_hi, n_lo, group, me_ref, table_ref, first_ref, start_ref, *refs):
    q_refs = refs[:n_hi]
    kv_refs = refs[n_hi:n_hi + n_lo]
    out_ref, key_buf, value_buf, score_buf = refs[n_hi + n_lo:]
    me = me_ref[0]
    factor = math.log2(math.e) / math.sqrt(HEAD_DIM)
    key_buf[:CHUNK] = jnp.zeros((CHUNK, HEAD_DIM), key_buf.dtype)
    value_buf[:CHUNK] = jnp.zeros((CHUNK, HEAD_DIM), value_buf.dtype)
    for lo in range(n_lo):
        for hi in range(n_hi):
            for slot in range(2):
                at = table_ref[me ^ (hi * n_lo + lo), slot] * group + CHUNK
                at = pl.multiple_of(at, group)
                rows = pl.ds(slot * group, group)
                key_buf[pl.ds(at, group)] = kv_refs[lo][hi, 0, rows]
                value_buf[pl.ds(at, group)] = kv_refs[lo][hi, 1, rows]

    lane = lax.broadcasted_iota(jnp.int32, (group, CHUNK), 1)
    row = lax.broadcasted_iota(jnp.int32, (group, CHUNK), 0)
    lanes = CHUNK // HEAD_DIM

    def by_lane(op, x):
        total = x[:, :HEAD_DIM]
        for i in range(1, lanes):
            total = op(total, x[:, i * HEAD_DIM:(i + 1) * HEAD_DIM])
        return total

    for hi in range(n_hi):
        for slot in range(2):
            number = table_ref[me ^ (hi * n_lo), slot]
            end = (number + 1) * group
            count = (end - first_ref[number] + CHUNK - 1) // CHUNK
            query = q_refs[hi][slot * group:(slot + 1) * group, :]
            starts = jnp.broadcast_to(start_ref[pl.ds(number, 1), :], (group, group)).T[:, :1]
            low = starts - lane
            high = row - lane + (end - group)

            def score(i, top):
                base = end - (i + 1) * CHUNK
                at = pl.multiple_of(base + CHUNK, group)
                s = lax.dot_general(
                    query, key_buf[pl.ds(at, CHUNK)],
                    (((1,), (1,)), ((), ())), preferred_element_type=jnp.float32,
                )
                s = jnp.where((low <= base) & (high >= base), s, HIDDEN)
                score_buf[i] = s
                return jnp.maximum(top, by_lane(jnp.maximum, s))

            top = lax.fori_loop(0, count, score, jnp.full((group, HEAD_DIM), HIDDEN, jnp.float32))
            top = jnp.max(top, axis=1, keepdims=True)

            def weigh(i, state):
                total, summed = state
                at = pl.multiple_of(end - i * CHUNK, group)
                w = jnp.exp2((score_buf[i] - top) * factor)
                total = total + by_lane(jnp.add, w)
                summed = summed + jnp.dot(
                    w.astype(jnp.bfloat16), value_buf[pl.ds(at, CHUNK)],
                    preferred_element_type=jnp.float32,
                )
                return total, summed

            zeros = jnp.zeros((group, HEAD_DIM), jnp.float32)
            total, summed = lax.fori_loop(0, count, weigh, (zeros, zeros))
            total = jnp.sum(total, axis=1, keepdims=True)
            out_ref[hi, slot * group:(slot + 1) * group, :] = (summed / total).astype(out_ref.dtype)


def shards(n_blk, queries, keys, values, group_table, doc_ids):
    tok_rows = queries.shape[0]
    group = tok_rows // 2
    n_hi = queries.shape[1] // HEAD_DIM
    n_lo = n_blk // n_hi
    seq = doc_ids.shape[0]
    me = lax.axis_index("blk")
    my_hi = me // n_lo

    def swap(x, by):
        return lax.ppermute(x, "blk", [(b, b ^ by) for b in range(n_blk)])

    def head_of(x, hi):
        return lax.dynamic_slice(x, (0, hi * HEAD_DIM), (tok_rows, HEAD_DIM))

    pieces = []
    for step in range(n_hi):
        piece = jnp.stack([head_of(x, my_hi ^ step) for x in (keys, values, queries)])
        pieces.append(swap(piece, step * n_lo) if step else piece)
    own = jnp.stack([piece[:2] for piece in pieces])
    held = {0: own}
    bit = n_lo // 2
    while bit:
        for j in list(held):
            held[j ^ bit] = swap(held[j], bit)
        bit //= 2

    table = lax.all_gather(group_table, "blk", axis=0, tiled=True)
    index = jnp.arange(seq, dtype=jnp.int32)
    before = jnp.concatenate([doc_ids[:1], doc_ids[:-1]])
    start = lax.cummax(jnp.where(doc_ids != before, index, 0))
    start = start.reshape(seq // group, group)

    smem = pl.BlockSpec(memory_space=pltpu.SMEM)
    vmem = pl.BlockSpec(memory_space=pltpu.VMEM)
    outs = pl.pallas_call(
        functools.partial(attend_kernel, n_hi, n_lo, group),
        out_shape=jax.ShapeDtypeStruct((n_hi, tok_rows, HEAD_DIM), jnp.bfloat16),
        in_specs=[smem] * 3 + [vmem] * (1 + n_hi + n_lo),
        out_specs=vmem,
        scratch_shapes=[
            pltpu.VMEM((seq + CHUNK, HEAD_DIM), jnp.bfloat16),
            pltpu.VMEM((seq + CHUNK, HEAD_DIM), jnp.bfloat16),
            pltpu.VMEM((seq // CHUNK, group, CHUNK), jnp.float32),
        ],
        name="attend",
    )(
        me.reshape(1), table, start[:, 0], start,
        *[piece[2] for piece in pieces], *[held[j] for j in range(n_lo)],
    )
    back = jnp.stack([swap(outs[j], j * n_lo) if j else outs[0] for j in range(n_hi)])
    heads = [lax.dynamic_index_in_dim(back, my_hi ^ h, 0, keepdims=False) for h in range(n_hi)]
    return jnp.concatenate(heads, axis=1)


def solution(mesh):
    in_specs = (P("blk", "head"), P("blk", "head"), P("blk", "head"), P("blk", None), P())
    out_specs = P("blk", "head")
    body = functools.partial(shards, mesh.shape["blk"])
    return jax.shard_map(body, mesh=mesh, in_specs=in_specs, out_specs=out_specs, check_vma=False)
```

time: 187 us -> 76.6 us (0.41)
  waiting for transfers between devices: 78.6 us -> 18.5 us
  local copies, waits for them, and re-layouts: 37.4 us -> 7.56 us
  between operations: 13.5 us -> 0.14 us
  matrix products: 12.7 us -> 0 us
  starting transfers between devices: 0.04 us -> 12.4 us
  loops' own time: 11.4 us -> 0 us
  Pallas kernels: 0 us -> 10.8 us
  other arithmetic: 9.23 us -> 2.06 us
    all_gather x2 -> x0, waiting for transfers between devices: 77.2 us -> none  [the longest x1 51.1 us: shards(): value_piece = lax.all_gather(values, 'blk', axis=0, tiled=True)]
    dynamic_slice x96 -> x0, local copies, waits for them, and re-layouts: 33.4 us -> none  [the longest x64 31 us: shards(): lax.scan(step, initial, (key_shards, value_shards, shard_ids))]
    ppermute x0 -> x9, waiting for transfers between devices: none -> 18.5 us  [swap(): return lax.ppermute(x, 'blk', [(b, b ^ by) for b in range(n_blk)])]
    dot_general x32 -> x0, matrix products: 12.7 us -> none  [the longest x16 6.68 us: attend_shard(): jnp.einsum('hqk,khd->qhd', weights.astype(jnp.bfloat16), value_heads, pre...]
    ppermute x0 -> x9, starting transfers between devices: none -> 12.4 us  [swap(): return lax.ppermute(x, 'blk', [(b, b ^ by) for b in range(n_blk)])]
    another operation x1 -> x0, loops' own time: 11.4 us -> none  [shards(): lax.scan(step, initial, (key_shards, value_shards, shard_ids))]
    pallas_call x0 -> x1, Pallas kernels: none -> 10.8 us  [shards(): pl.pallas_call(functools.partial(attend_kernel, n_hi, n_lo, group), out_s...]
    reduce_sum x16 -> x0, other arithmetic: 3.33 us -> none  [attend_shard(): weight_sum = weight_sum * factor + jnp.sum(weights, axis=-1)]
  transfers between devices with their start and end apart: 2 -> 9, of which waited for: 2 -> 6; matrix products, arithmetic and copies ran while one was open for 3% -> 6% of each run, Pallas kernels for 0% -> 0%
where the time goes in v1:
time: 76.6 us; the launch traced here: 75.6 us
  blocking collectives  24.2 us (32%)
  waiting for transfers between devices  18.5 us (24%)
  starting transfers between devices  12.4 us (16%)
  Pallas kernels  10.8 us (14%)
  local copies, waits for them, and re-layouts  7.56 us (10%)
  other arithmetic  2.06 us (3%)
    all_gather x1, blocking collectives, shards(): table = lax.all_gather(group_table, 'blk', axis=0, tiled=True)  24.2 us
    ppermute x9, waiting for transfers between devices, swap(): return lax.ppermute(x, 'blk', [(b, b ^ by) for b in range(n_blk)])  18.5 us
    ppermute x9, starting transfers between devices, swap(): return lax.ppermute(x, 'blk', [(b, b ^ by) for b in range(n_blk)])  12.4 us
    pallas_call x1, Pallas kernels, shards(): pl.pallas_call(functools.partial(attend_kernel, n_hi, n_lo, group), out_s...  10.8 us
    squeeze x3, local copies, waits for them, and re-layouts, shards(): piece[2]  1.97 us
    another operation x2, local copies, waits for them, and re-layouts, shards(): jnp.stack([head_of(x, my_hi ^ step) for x in (keys, values, queries)])  1.74 us
  transfers between devices with their start and end apart: 9, of which 6 were waited for; matrix products, arithmetic and copies ran while one was open for 6% of the time, Pallas kernels for 0%

profile of v1, /device:TPU:0, one launch (start us, length us, event | category | flops | bytes accessed | tf_op | source)
XLA Modules:
  0.0 75.6 jit_solution(2187538077547718207)
XLA Ops:
  0.0 1.6 %dynamic-slice_bitcast_fusion.6 = (bf16[1,256,128]{2,1,0:T(8,128)(2,1)S(1)}, bf16[1,256,128]{2,1,0:T(8,128)(2,1)S(1)}, bf16[256,128]{1,0:T(8,128)(2,1)}, bf16[1,256,128]{2,1,0:T(8,128)(2,1)S(1)}) fusion(bf16[256,512]{1,0:T(8,128)(2,1)} %param.5, s32[]{:T(128)S(6)} %select_n.47, s32[]{:T(128)S(6)} %select_n.45, s32[]{:T(128)S(6)} %select_n.44, s32[]{:T(128)S(6)} %select_n.46), kind=kLoop, calls=%fused_computation.22 | loop fusion | bytes 524304 | tf_op jit(solution)/shard_map/stack | solution.py:101
  1.7 0.0 copy-done.4
  1.7 0.0 copy-done.5
  1.7 0.1 dynamic-slice_bitcast_fusion.4
  1.8 5.1 %collective-permute-start.2 = (bf16[3,256,128]{2,1,0:T(8,128)(2,1)S(1)}, bf16[3,256,128]{2,1,0:T(8,128)(2,1)S(1)}, u32[]{:S(2)}, u32[]{:S(2)}) collective-permute-start(bf16[3,256,128]{2,1,0:T(8,128)(2,1)S(1)} %pad_maximum_fusion.5), channel_id=1, source_target_pairs={{0,24},{2,26},{4,28},{6,30},{8,16},{10,18},{12,20},{14,22},{16,8},... | collective-permute-start | bytes 589832 | tf_op jit(solution)/shard_map/ppermute | solution.py:94
  7.0 0.1 collective-permute-start
  7.0 0.0 copy-start.7
  7.1 0.6 collective-permute-start.1
  7.7 0.1 copy-done.7
  7.8 0.5 slice.46
  8.3 4.4 %collective-permute-done.2 = bf16[3,256,128]{2,1,0:T(8,128)(2,1)S(1)} collective-permute-done((bf16[3,256,128]{2,1,0:T(8,128)(2,1)S(1)}, bf16[3,256,128]{2,1,0:T(8,128)(2,1)S(1)}, u32[]{:S(2)}, u32[]{:S(2)}) %collective-permute-start.2) | collective-permute-done | bytes 196640 | tf_op jit(solution)/shard_map/ppermute | solution.py:94
  12.7 4.4 %collective-permute-done = bf16[3,256,128]{2,1,0:T(8,128)(2,1)S(1)} collective-permute-done((bf16[3,256,128]{2,1,0:T(8,128)(2,1)S(1)}, bf16[3,256,128]{2,1,0:T(8,128)(2,1)S(1)}, u32[]{:S(2)}, u32[]{:S(2)}) %collective-permute-start) | collective-permute-done | bytes 196640 | tf_op jit(solution)/shard_map/ppermute | solution.py:94
  17.1 6.5 %collective-permute-done.1 = bf16[3,256,128]{2,1,0:T(8,128)(2,1)S(1)} collective-permute-done((bf16[3,256,128]{2,1,0:T(8,128)(2,1)S(1)}, bf16[3,256,128]{2,1,0:T(8,128)(2,1)S(1)}, u32[]{:S(2)}, u32[]{:S(2)}) %collective-permute-start.1) | collective-permute-done | bytes 196640 | tf_op jit(solution)/shard_map/ppermute | solution.py:94
  23.6 0.1 pad_maximum_fusion.refs_4_
  23.7 0.0 copy-start
  23.7 1.6 %collective-permute-start.4 = (bf16[4,2,256,128]{3,2,1,0:T(8,128)(2,1)S(1)}, bf16[4,2,256,128]{3,2,1,0:T(8,128)(2,1)S(1)}, u32[]{:S(2)}, u32[]{:S(2)}) collective-permute-start(bf16[4,2,256,128]{3,2,1,0:T(8,128)(2,1)S(1)} %pad_maximum_fusion.refs_4_), channel_id=1, source_target_pairs={{0,4},{2,6},{4,0},{6,2},{8,12},{10,14},{12,8},{14,10},{16,20},{18,... | collective-permute-start | bytes 1572872 | tf_op jit(solution)/shard_map/ppermute | solution.py:94
  25.3 0.7 select_bitcast_fusion
  26.0 0.3 reduce-window.9
  26.3 0.1 slice.61
  26.4 0.1 reduce-window.12
  26.5 0.0 copy-start.8
  26.5 0.6 copy-done.8
  27.1 24.2 %all-gather = s32[16,1,2]{2,1,0:T(1,128)} all-gather(s32[1,1,2]{2,1,0:T(1,128)S(1)} %bitcast.64), channel_id=1, replica_groups=mesh['blk'=16,'head'=2] {'blk'}, dimensions={0}, use_global_device_ids=true | all-gather | bytes 136 | tf_op jit(solution)/shard_map/all_gather | solution.py:111
  51.3 0.1 slice_reduce_fusion.1
  51.4 0.1 broadcast_maximum_fusion.start_ref
  51.5 0.6 slice_reduce_fusion.first_ref
  52.1 0.3 collective-permute-start.3
  52.4 0.0 collective-permute-done.4.refs_6_
  52.4 0.2 collective-permute-start.5
  52.6 0.7 slice_bitcast_fusion.6.refs_3_
  53.3 0.0 copy-done.6
  53.3 0.6 slice_bitcast_fusion.8.refs_1_
  53.9 0.6 slice_bitcast_fusion.7.refs_2_
  54.6 0.0 collective-permute-done.3.refs_5_
  54.6 0.2 collective-permute-done.5.refs_7_
  54.7 0.0 copy-done
  54.7 0.0 copy-done.1
  54.7 0.6 copy-done.2
  55.4 0.2 copy-done.3
  55.5 10.8 %attend.1 = bf16[4,256,128]{2,1,0:T(8,128)(2,1)} custom-call(s32[1]{0:T(128)} %bitcast.me_ref, s32[16,2]{1,0:T(8,128)} %bitcast.63, s32[32]{0:T(128)} %slice_reduce_fusion.first_ref, s32[32,128]{1,0:T(8,128)} %copy-done.6, bf16[256,128]{1,0:T(8,128)(2,1)} %get-tuple-element.23.refs_0_, bf16[256,128]{1,0:T(8,128)(2,1)} %slice_bitcast_fusion.8.refs_1_, ...), custom_call_target="tpu_custom_call" | custom-call | tf_op jit(solution)/shard_map/attend/pallas_call | solution.py:119
  66.4 1.0 %fusion = (bf16[1,256,128]{2,1,0:T(8,128)(2,1)S(1)}, bf16[256,128]{1,0:T(8,128)(2,1)S(1)}, bf16[256,128]{1,0:T(8,128)(2,1)S(1)}, bf16[256,128]{1,0:T(8,128)(2,1)S(1)}) fusion(bf16[4,256,128]{2,1,0:T(8,128)(2,1)} %attend.1), kind=kLoop, calls=%fused_computation.37 | loop fusion | bytes 524288 | tf_op jit(solution)/shard_map/slice | solution.py:134
  67.3 0.1 collective-permute-start.8
  67.4 0.1 collective-permute-start.7
  67.5 4.3 %collective-permute-start.6 = (bf16[256,128]{1,0:T(8,128)(2,1)S(1)}, bf16[256,128]{1,0:T(8,128)(2,1)S(1)}, u32[]{:S(2)}, u32[]{:S(2)}) collective-permute-start(bf16[256,128]{1,0:T(8,128)(2,1)S(1)} %get-tuple-element.12), channel_id=1, source_target_pairs={{0,8},{2,10},{4,12},{6,14},{8,0},{10,2},{12,4},{14,6},{16,24},{18,... | collective-permute-start | bytes 196616 | tf_op jit(solution)/shard_map/ppermute | solution.py:94
  71.8 2.3 %collective-permute-done.8 = bf16[256,128]{1,0:T(8,128)(2,1)S(1)} collective-permute-done((bf16[256,128]{1,0:T(8,128)(2,1)S(1)}, bf16[256,128]{1,0:T(8,128)(2,1)S(1)}, u32[]{:S(2)}, u32[]{:S(2)}) %collective-permute-start.8) | collective-permute-done | bytes 65568 | tf_op jit(solution)/shard_map/ppermute | solution.py:94
  74.1 0.0 collective-permute-done.7
  74.1 0.7 collective-permute-done.6
  74.9 0.7 pad_maximum_fusion.2
  (15 shorter events, 0.2 us)
Async XLA Ops:
  0.0 1.7 %copy-start.4 = (bf16[256,512]{1,0:T(8,128)(2,1)S(1)}, bf16[256,512]{1,0:T(8,128)(2,1)}, u32[]{:S(2)}) copy-start(bf16[256,512]{1,0:T(8,128)(2,1)} %param.7) | copy-start | bytes 786436
  0.0 1.7 %copy-start.5 = (bf16[256,512]{1,0:T(8,128)(2,1)S(1)}, bf16[256,512]{1,0:T(8,128)(2,1)}, u32[]{:S(2)}) copy-start(bf16[256,512]{1,0:T(8,128)(2,1)} %param.6) | copy-start | bytes 786436
  1.8 10.9 %collective-permute-start.2 = (bf16[3,256,128]{2,1,0:T(8,128)(2,1)S(1)}, bf16[3,256,128]{2,1,0:T(8,128)(2,1)S(1)}, u32[]{:S(2)}, u32[]{:S(2)}) collective-permute-start(bf16[3,256,128]{2,1,0:T(8,128)(2,1)S(1)} %pad_maximum_fusion.5), channel_id=1, source_target_pairs={{0,24},{2,26},{4,28},{6,30},{8,16},{10,18},{12,20},{14,22},{16,8},... | collective-permute-start | bytes 589832 | tf_op jit(solution)/shard_map/ppermute | solution.py:94
  7.0 10.1 %collective-permute-start = (bf16[3,256,128]{2,1,0:T(8,128)(2,1)S(1)}, bf16[3,256,128]{2,1,0:T(8,128)(2,1)S(1)}, u32[]{:S(2)}, u32[]{:S(2)}) collective-permute-start(bf16[3,256,128]{2,1,0:T(8,128)(2,1)S(1)} %pad_maximum_fusion.3), channel_id=1, source_target_pairs={{0,8},{2,10},{4,12},{6,14},{8,0},{10,2},{12,4},{14,6},{16,24},{18,... | collective-permute-start | bytes 589832 | tf_op jit(solution)/shard_map/ppermute | solution.py:94
  7.0 0.7 copy-start.7
  7.1 16.5 %collective-permute-start.1 = (bf16[3,256,128]{2,1,0:T(8,128)(2,1)S(1)}, bf16[3,256,128]{2,1,0:T(8,128)(2,1)S(1)}, u32[]{:S(2)}, u32[]{:S(2)}) collective-permute-start(bf16[3,256,128]{2,1,0:T(8,128)(2,1)S(1)} %pad_maximum_fusion.4), channel_id=1, source_target_pairs={{0,16},{2,18},{4,20},{6,22},{8,24},{10,26},{12,28},{14,30},{16,0},... | collective-permute-start | bytes 589832 | tf_op jit(solution)/shard_map/ppermute | solution.py:94
  23.7 31.0 %copy-start = (bf16[4,2,256,128]{3,2,1,0:T(8,128)(2,1)}, bf16[4,2,256,128]{3,2,1,0:T(8,128)(2,1)S(1)}, u32[]{:S(2)}) copy-start(bf16[4,2,256,128]{3,2,1,0:T(8,128)(2,1)S(1)} %pad_maximum_fusion.refs_4_) | copy-start | bytes 1572868
  23.7 28.7 %collective-permute-start.4 = (bf16[4,2,256,128]{3,2,1,0:T(8,128)(2,1)S(1)}, bf16[4,2,256,128]{3,2,1,0:T(8,128)(2,1)S(1)}, u32[]{:S(2)}, u32[]{:S(2)}) collective-permute-start(bf16[4,2,256,128]{3,2,1,0:T(8,128)(2,1)S(1)} %pad_maximum_fusion.refs_4_), channel_id=1, source_target_pairs={{0,4},{2,6},{4,0},{6,2},{8,12},{10,14},{12,8},{14,10},{16,20},{18,... | collective-permute-start | bytes 1572872 | tf_op jit(solution)/shard_map/ppermute | solution.py:94
  26.5 0.7 copy-start.8
  51.5 1.9 %copy-start.6 = (s32[32,128]{1,0:T(8,128)}, s32[32,128]{1,0:T(8,128)S(1)}, u32[]{:S(2)}) copy-start(s32[32,128]{1,0:T(8,128)S(1)} %broadcast_maximum_fusion.start_ref) | copy-start | bytes 49156
  52.1 2.5 %collective-permute-start.3 = (bf16[4,2,256,128]{3,2,1,0:T(8,128)(2,1)S(1)}, bf16[4,2,256,128]{3,2,1,0:T(8,128)(2,1)S(1)}, u32[]{:S(2)}, u32[]{:S(2)}) collective-permute-start(bf16[4,2,256,128]{3,2,1,0:T(8,128)(2,1)S(1)} %pad_maximum_fusion.refs_4_), channel_id=1, source_target_pairs={{0,2},{2,0},{4,6},{6,4},{8,10},{10,8},{12,14},{14,12},{16,18},{18,... | collective-permute-start | bytes 1572872 | tf_op jit(solution)/shard_map/ppermute | solution.py:94
  52.4 2.3 %copy-start.1 = (bf16[4,2,256,128]{3,2,1,0:T(8,128)(2,1)}, bf16[4,2,256,128]{3,2,1,0:T(8,128)(2,1)S(1)}, u32[]{:S(2)}) copy-start(bf16[4,2,256,128]{3,2,1,0:T(8,128)(2,1)S(1)} %collective-permute-done.4.refs_6_) | copy-start | bytes 1572868
  52.4 2.3 %collective-permute-start.5 = (bf16[4,2,256,128]{3,2,1,0:T(8,128)(2,1)S(1)}, bf16[4,2,256,128]{3,2,1,0:T(8,128)(2,1)S(1)}, u32[]{:S(2)}, u32[]{:S(2)}) collective-permute-start(bf16[4,2,256,128]{3,2,1,0:T(8,128)(2,1)S(1)} %collective-permute-done.4.refs_6_), channel_id=1, source_target_pairs={{0,2},{2,0},{4,6},{6,4},{8,10},{10,8},{12,14},{14,12},{16,18},{18,... | collective-permute-start | bytes 1572872 | tf_op jit(solution)/shard_map/ppermute | solution.py:94
  54.6 0.8 %copy-start.2 = (bf16[4,2,256,128]{3,2,1,0:T(8,128)(2,1)}, bf16[4,2,256,128]{3,2,1,0:T(8,128)(2,1)S(1)}, u32[]{:S(2)}) copy-start(bf16[4,2,256,128]{3,2,1,0:T(8,128)(2,1)S(1)} %collective-permute-done.3.refs_5_) | copy-start | bytes 1572868
  54.7 0.8 %copy-start.3 = (bf16[4,2,256,128]{3,2,1,0:T(8,128)(2,1)}, bf16[4,2,256,128]{3,2,1,0:T(8,128)(2,1)S(1)}, u32[]{:S(2)}) copy-start(bf16[4,2,256,128]{3,2,1,0:T(8,128)(2,1)S(1)} %collective-permute-done.5.refs_7_) | copy-start | bytes 1572868
  67.3 6.8 %collective-permute-start.8 = (bf16[256,128]{1,0:T(8,128)(2,1)S(1)}, bf16[256,128]{1,0:T(8,128)(2,1)S(1)}, u32[]{:S(2)}, u32[]{:S(2)}) collective-permute-start(bf16[256,128]{1,0:T(8,128)(2,1)S(1)} %get-tuple-element.10), channel_id=1, source_target_pairs={{0,24},{2,26},{4,28},{6,30},{8,16},{10,18},{12,20},{14,22},{16,8},... | collective-permute-start | bytes 196616 | tf_op jit(solution)/shard_map/ppermute | solution.py:94
  67.4 6.7 %collective-permute-start.7 = (bf16[256,128]{1,0:T(8,128)(2,1)S(1)}, bf16[256,128]{1,0:T(8,128)(2,1)S(1)}, u32[]{:S(2)}, u32[]{:S(2)}) collective-permute-start(bf16[256,128]{1,0:T(8,128)(2,1)S(1)} %get-tuple-element.11), channel_id=1, source_target_pairs={{0,16},{2,18},{4,20},{6,22},{8,24},{10,26},{12,28},{14,30},{16,0},... | collective-permute-start | bytes 196616 | tf_op jit(solution)/shard_map/ppermute | solution.py:94
  67.5 7.3 %collective-permute-start.6 = (bf16[256,128]{1,0:T(8,128)(2,1)S(1)}, bf16[256,128]{1,0:T(8,128)(2,1)S(1)}, u32[]{:S(2)}, u32[]{:S(2)}) collective-permute-start(bf16[256,128]{1,0:T(8,128)(2,1)S(1)} %get-tuple-element.12), channel_id=1, source_target_pairs={{0,8},{2,10},{4,12},{6,14},{8,0},{10,2},{12,4},{14,6},{16,24},{18,... | collective-permute-start | bytes 196616 | tf_op jit(solution)/shard_map/ppermute | solution.py:94

commit v2 on v1

--- a/solution.py
+++ b/solution.py
@@ -11,24 +11,37 @@
 HEAD_DIM = 128
 CHUNK = 512
 HIDDEN = -1e30
+NOTE_ROWS = 16
 
 
-def attend_kernel(n_hi, n_lo, group, me_ref, table_ref, first_ref, start_ref, *refs):
-    q_refs = refs[:n_hi]
-    kv_refs = refs[n_hi:n_hi + n_lo]
-    out_ref, key_buf, value_buf, score_buf = refs[n_hi + n_lo:]
-    me = me_ref[0]
+def attend_kernel(n_hi, n_lo, group, first_ref, start_ref, *refs):
+    tok_rows = 2 * group
+    piece_refs = refs[:n_hi]
+    held_refs = refs[n_hi:n_hi + n_lo - 1]
+    out_refs = refs[n_hi + n_lo - 1:2 * n_hi + n_lo - 1]
+    key_buf, value_buf, score_buf = refs[2 * n_hi + n_lo - 1:]
     factor = math.log2(math.e) / math.sqrt(HEAD_DIM)
+
+    def stored(hi, lo, first, count):
+        rows = slice(first, first + count)
+        return held_refs[lo - 1][hi, rows] if lo else piece_refs[hi][rows]
+
+    def group_numbers(hi, lo):
+        notes = stored(hi, lo, 2 * tok_rows, NOTE_ROWS).astype(jnp.float32).astype(jnp.int32)
+        return notes[0, 0], notes[NOTE_ROWS // 2, 0]
+
     key_buf[:CHUNK] = jnp.zeros((CHUNK, HEAD_DIM), key_buf.dtype)
     value_buf[:CHUNK] = jnp.zeros((CHUNK, HEAD_DIM), value_buf.dtype)
+    mine = []
     for lo in range(n_lo):
         for hi in range(n_hi):
+            numbers = group_numbers(hi, lo)
+            if lo == 0:
+                mine.append(numbers)
             for slot in range(2):
-                at = table_ref[me ^ (hi * n_lo + lo), slot] * group + CHUNK
-                at = pl.multiple_of(at, group)
-                rows = pl.ds(slot * group, group)
-                key_buf[pl.ds(at, group)] = kv_refs[lo][hi, 0, rows]
-                value_buf[pl.ds(at, group)] = kv_refs[lo][hi, 1, rows]
+                at = pl.multiple_of(numbers[slot] * group + CHUNK, group)
+                key_buf[pl.ds(at, group)] = stored(hi, lo, slot * group, group)
+                value_buf[pl.ds(at, group)] = stored(hi, lo, tok_rows + slot * group, group)
 
     lane = lax.broadcasted_iota(jnp.int32, (group, CHUNK), 1)
     row = lax.broadcasted_iota(jnp.int32, (group, CHUNK), 0)
@@ -42,10 +55,11 @@
 
     for hi in range(n_hi):
         for slot in range(2):
-            number = table_ref[me ^ (hi * n_lo), slot]
+            number = mine[hi][slot]
             end = (number + 1) * group
             count = (end - first_ref[number] + CHUNK - 1) // CHUNK
-            query = q_refs[hi][slot * group:(slot + 1) * group, :]
+            q_row = 2 * tok_rows + NOTE_ROWS + slot * group
+            query = piece_refs[hi][q_row:q_row + group, :]
             starts = jnp.broadcast_to(start_ref[pl.ds(number, 1), :], (group, group)).T[:, :1]
             low = starts - lane
             high = row - lane + (end - group)
@@ -78,7 +92,7 @@
             zeros = jnp.zeros((group, HEAD_DIM), jnp.float32)
             total, summed = lax.fori_loop(0, count, weigh, (zeros, zeros))
             total = jnp.sum(total, axis=1, keepdims=True)
-            out_ref[hi, slot * group:(slot + 1) * group, :] = (summed / total).astype(out_ref.dtype)
+            out_refs[hi][slot * group:(slot + 1) * group, :] = (summed / total).astype(jnp.bfloat16)
 
 
 def shards(n_blk, queries, keys, values, group_table, doc_ids):
@@ -87,6 +101,7 @@
     n_hi = queries.shape[1] // HEAD_DIM
     n_lo = n_blk // n_hi
     seq = doc_ids.shape[0]
+    assert seq // group <= 256
     me = lax.axis_index("blk")
     my_hi = me // n_lo
 
@@ -96,11 +111,15 @@
     def head_of(x, hi):
         return lax.dynamic_slice(x, (0, hi * HEAD_DIM), (tok_rows, HEAD_DIM))
 
+    notes = jnp.repeat(group_table[0], NOTE_ROWS // 2).astype(jnp.bfloat16)
+    notes = jnp.broadcast_to(notes[:, None], (NOTE_ROWS, HEAD_DIM))
+    kv_rows = 2 * tok_rows + NOTE_ROWS
     pieces = []
     for step in range(n_hi):
-        piece = jnp.stack([head_of(x, my_hi ^ step) for x in (keys, values, queries)])
+        hi = my_hi ^ step
+        piece = jnp.concatenate([head_of(keys, hi), head_of(values, hi), notes, head_of(queries, hi)])
         pieces.append(swap(piece, step * n_lo) if step else piece)
-    own = jnp.stack([piece[:2] for piece in pieces])
+    own = jnp.stack([piece[:kv_rows] for piece in pieces])
     held = {0: own}
     bit = n_lo // 2
     while bit:
@@ -108,7 +127,6 @@
             held[j ^ bit] = swap(held[j], bit)
         bit //= 2
 
-    table = lax.all_gather(group_table, "blk", axis=0, tiled=True)
     index = jnp.arange(seq, dtype=jnp.int32)
     before = jnp.concatenate([doc_ids[:1], doc_ids[:-1]])
     start = lax.cummax(jnp.where(doc_ids != before, index, 0))
@@ -118,9 +136,9 @@
     vmem = pl.BlockSpec(memory_space=pltpu.VMEM)
     outs = pl.pallas_call(
         functools.partial(attend_kernel, n_hi, n_lo, group),
-        out_shape=jax.ShapeDtypeStruct((n_hi, tok_rows, HEAD_DIM), jnp.bfloat16),
-        in_specs=[smem] * 3 + [vmem] * (1 + n_hi + n_lo),
-        out_specs=vmem,
+        out_shape=[jax.ShapeDtypeStruct((tok_rows, HEAD_DIM), jnp.bfloat16)] * n_hi,
+        in_specs=[smem] + [vmem] * (n_hi + n_lo),
+        out_specs=[vmem] * n_hi,
         scratch_shapes=[
             pltpu.VMEM((seq + CHUNK, HEAD_DIM), jnp.bfloat16),
             pltpu.VMEM((seq + CHUNK, HEAD_DIM), jnp.bfloat16),
@@ -128,8 +146,7 @@
         ],
         name="attend",
     )(
-        me.reshape(1), table, start[:, 0], start,
-        *[piece[2] for piece in pieces], *[held[j] for j in range(n_lo)],
+        start[:, 0], start, *pieces, *[held[j] for j in range(1, n_lo)],
     )
     back = jnp.stack([swap(outs[j], j * n_lo) if j else outs[0] for j in range(n_hi)])
     heads = [lax.dynamic_index_in_dim(back, my_hi ^ h, 0, keepdims=False) for h in range(n_hi)]

time: 76.6 us -> 64.3 us (0.84)
  blocking collectives: 24.2 us -> 0 us
  waiting for transfers between devices: 18.5 us -> 31.6 us
  local copies, waits for them, and re-layouts: 7.56 us -> 5.11 us
  other arithmetic: 2.06 us -> 3.46 us
  Pallas kernels: 10.8 us -> 12 us
  starting transfers between devices: 12.4 us -> 11.6 us
    all_gather x1 -> x0, blocking collectives: 24.2 us -> none  [shards(): table = lax.all_gather(group_table, 'blk', axis=0, tiled=True)]
    ppermute x9, waiting for transfers between devices: 18.5 us -> 31.6 us  [swap(): return lax.ppermute(x, 'blk', [(b, b ^ by) for b in range(n_blk)])]
    squeeze x3 -> x0, local copies, waits for them, and re-layouts: 1.97 us -> none  [shards(): piece[2]]
    another operation x6 -> x4, local copies, waits for them, and re-layouts: 1.88 us -> 0.14 us  [the longest x2 1.74 us: shards(): jnp.stack([head_of(x, my_hi ^ step) for x in (keys, values, queries)])]
    pallas_call x1, Pallas kernels: 10.8 us -> 12 us  [shards(): pl.pallas_call(functools.partial(attend_kernel, n_hi, n_lo, group), out_s...]
    dynamic_slice x0 -> x2, local copies, waits for them, and re-layouts: none -> 1.11 us  [head_of(): return lax.dynamic_slice(x, (0, hi * HEAD_DIM), (tok_rows, HEAD_DIM))]
    slice x2 -> x1, local copies, waits for them, and re-layouts: 1.03 us -> 0.08 us  [the longest x1 0.95 us: shards(): outs[0]]
    unnamed x18 -> x22, local copies, waits for them, and re-layouts: 1.52 us -> 2.39 us
  transfers between devices with their start and end apart: 9 -> 9, of which waited for: 6 -> 6; matrix products, arithmetic and copies ran while one was open for 6% -> 4% of each run, Pallas kernels for 0% -> 0%
where the time goes in v2:
time: 64.3 us; the launch traced here: 63.8 us
  waiting for transfers between devices  31.6 us (49%)
  Pallas kernels  12 us (19%)
  starting transfers between devices  11.6 us (18%)
  local copies, waits for them, and re-layouts  5.11 us (8%)
  other arithmetic  3.46 us (5%)
    ppermute x9, waiting for transfers between devices, swap(): return lax.ppermute(x, 'blk', [(b, b ^ by) for b in range(n_blk)])  31.6 us
    pallas_call x1, Pallas kernels, shards(): pl.pallas_call(functools.partial(attend_kernel, n_hi, n_lo, group), out_s...  12 us
    ppermute x9, starting transfers between devices, swap(): return lax.ppermute(x, 'blk', [(b, b ^ by) for b in range(n_blk)])  11.6 us
    unnamed x22, local copies, waits for them, and re-layouts  2.39 us
  transfers between devices with their start and end apart: 9, of which 6 were waited for; matrix products, arithmetic and copies ran while one was open for 4% of the time, Pallas kernels for 0%

profile of v2, /device:TPU:0, one launch (start us, length us, event | category | flops | bytes accessed | tf_op | source)
XLA Modules:
  0.0 63.8 jit_solution(8001480878496286812)
XLA Ops:
  0.0 0.7 %copy-done.10 = s32[1,2]{1,0:T(1,128)S(1)} copy-done((s32[1,2]{1,0:T(1,128)S(1)}, s32[1,2]{1,0:T(1,128)}, u32[]{:S(2)}) %copy-start.10) | copy-done | bytes 32
  0.7 0.1 broadcast_in_dim.14
  0.7 0.1 convert_element_type.16
  0.8 1.0 %constant_dynamic-slice_fusion.2 = (bf16[256,128]{1,0:T(8,128)(2,1)S(1)}, bf16[256,128]{1,0:T(8,128)(2,1)S(1)}, bf16[256,128]{1,0:T(8,128)(2,1)S(1)}, bf16[256,128]{1,0:T(8,128)(2,1)S(1)}) fusion(bf16[256,512]{1,0:T(8,128)(2,1)} %param.6, s32[]{:T(128)S(6)} %select_n.47, s32[]{:T(128)S(6)} %select_n.45, s32[]{:T(128)S(6)} %select_n.44, s32[]{:T(128)S(6)} %select_n.46), kind=kLoop, calls=%fused_computation.26 | loop fusion | bytes 524304 | tf_op jit(solution)/shard_map/dynamic_slice | solution.py:112
  1.8 0.1 copy-done.6
  1.9 0.1 copy-done.7
  2.0 0.1 constant_dynamic-slice_fusion
  2.1 0.1 broadcast_in_dim.15
  2.2 0.7 %fusion.3 = (bf16[784,128]{1,0:T(8,128)(2,1)S(1)}, bf16[784,128]{1,0:T(8,128)(2,1)S(1)}, bf16[784,128]{1,0:T(8,128)(2,1)S(1)}, bf16[784,128]{1,0:T(8,128)(2,1)}) fusion(bf16[16,128]{1,0:T(8,128)(2,1)S(1)} %broadcast_in_dim.15, bf16[256,128]{1,0:T(8,128)(2,1)S(1)} %get-tuple-element.25, bf16[256,128]{1,0:T(8,128)(2,1)S(1)} %get-tuple-element.36, ...), kind=kLoop, calls=%fused_computation.10 | loop fusion | flops 2910208 | bytes 1593344 | tf_op jit(solution)/shard_map/concatenate | solution.py:120
  2.9 5.1 %collective-permute-start.2 = (bf16[784,128]{1,0:T(8,128)(2,1)S(1)}, bf16[784,128]{1,0:T(8,128)(2,1)S(1)}, u32[]{:S(2)}, u32[]{:S(2)}) collective-permute-start(bf16[784,128]{1,0:T(8,128)(2,1)S(1)} %get-tuple-element.29), channel_id=1, source_target_pairs={{0,24},{2,26},{4,28},{6,30},{8,16},{10,18},{12,20},{14,22},{16,8},... | collective-permute-start | bytes 602120 | tf_op jit(solution)/shard_map/ppermute | solution.py:109
  8.0 0.0 collective-permute-start
  8.0 0.6 collective-permute-start.1
  8.5 5.3 %collective-permute-done.2.refs_3_ = bf16[784,128]{1,0:T(8,128)(2,1)S(1)} collective-permute-done((bf16[784,128]{1,0:T(8,128)(2,1)S(1)}, bf16[784,128]{1,0:T(8,128)(2,1)S(1)}, u32[]{:S(2)}, u32[]{:S(2)}) %collective-permute-start.2) | collective-permute-done | bytes 200736 | tf_op jit(solution)/shard_map/ppermute | solution.py:109
  13.9 11.1 %collective-permute-done.1.refs_2_ = bf16[784,128]{1,0:T(8,128)(2,1)S(1)} collective-permute-done((bf16[784,128]{1,0:T(8,128)(2,1)S(1)}, bf16[784,128]{1,0:T(8,128)(2,1)S(1)}, u32[]{:S(2)}, u32[]{:S(2)}) %collective-permute-start.1) | collective-permute-done | bytes 200736 | tf_op jit(solution)/shard_map/ppermute | solution.py:109
  25.0 0.0 copy-done
  25.0 0.0 collective-permute-done.refs_1_
  25.0 0.0 copy-start.1
  25.1 0.6 copy-done.2
  25.7 0.1 pad_maximum_fusion
  25.8 0.0 copy-done.1
  25.8 1.6 %collective-permute-start.4 = (bf16[4,528,128]{2,1,0:T(8,128)(2,1)S(1)}, bf16[4,528,128]{2,1,0:T(8,128)(2,1)S(1)}, u32[]{:S(2)}, u32[]{:S(2)}) collective-permute-start(bf16[4,528,128]{2,1,0:T(8,128)(2,1)S(1)} %pad_maximum_fusion), channel_id=1, source_target_pairs={{0,4},{2,6},{4,0},{6,2},{8,12},{10,14},{12,8},{14,10},{16,20},{18,... | collective-permute-start | bytes 1622024 | tf_op jit(solution)/shard_map/ppermute | solution.py:109
  27.4 0.0 copy-done.9
  27.4 0.5 slice.27
  27.9 0.0 collective-permute-start.3
  27.9 11.3 %collective-permute-done.4.refs_5_ = bf16[4,528,128]{2,1,0:T(8,128)(2,1)S(1)} collective-permute-done((bf16[4,528,128]{2,1,0:T(8,128)(2,1)S(1)}, bf16[4,528,128]{2,1,0:T(8,128)(2,1)S(1)}, u32[]{:S(2)}, u32[]{:S(2)}) %collective-permute-start.4) | collective-permute-done | bytes 540704 | tf_op jit(solution)/shard_map/ppermute | solution.py:109
  39.2 0.0 collective-permute-start.5
  39.2 0.6 select_bitcast_fusion
  39.8 0.3 reduce-window.9
  40.1 0.1 slice.35
  40.2 0.1 reduce-window.12
  40.2 0.1 slice_reduce_fusion.1
  40.4 0.1 broadcast_maximum_fusion.start_ref
  40.4 0.6 %slice_reduce_fusion.first_ref = s32[32]{0:T(128)} fusion(s32[32,128]{1,0:T(8,128)S(1)} %broadcast_maximum_fusion.start_ref), kind=kLoop, calls=%fused_computation.19 | loop fusion | bytes 256 | tf_op jit(solution)/shard_map/slice | solution.py:149
  41.1 0.0 collective-permute-done.3.refs_4_
  41.1 0.1 collective-permute-done.5.refs_6_
  41.1 0.0 copy-done.3
  41.1 0.0 copy-done.8
  41.1 0.7 %copy-done.4 = bf16[4,528,128]{2,1,0:T(8,128)(2,1)} copy-done((bf16[4,528,128]{2,1,0:T(8,128)(2,1)}, bf16[4,528,128]{2,1,0:T(8,128)(2,1)S(1)}, u32[]{:S(2)}) %copy-start.4) | copy-done | bytes 540696
  41.9 0.2 copy-done.5
  42.1 12.0 %attend.1 = (bf16[256,128]{1,0:T(8,128)(2,1)}, bf16[256,128]{1,0:T(8,128)(2,1)}, bf16[256,128]{1,0:T(8,128)(2,1)}, bf16[256,128]{1,0:T(8,128)(2,1)}) custom-call(s32[32]{0:T(128)} %slice_reduce_fusion.first_ref, s32[32,128]{1,0:T(8,128)} %copy-done.8, bf16[784,128]{1,0:T(8,128)(2,1)} %get-tuple-element.32.refs_0_, bf16[784,128]{1,0:T(8,128)(2,1)} %copy-done.1, ...), custom_call_target="tpu_custom_call" | custom-call | tf_op jit(solution)/shard_map/attend/pallas_call | solution.py:137
  54.1 2.3 %collective-permute-start.8 = (bf16[256,128]{1,0:T(8,128)(2,1)}, bf16[256,128]{1,0:T(8,128)(2,1)S(1)}, u32[]{:S(2)}, u32[]{:S(2)}) collective-permute-start(bf16[256,128]{1,0:T(8,128)(2,1)} %get-tuple-element.12), channel_id=1, source_target_pairs={{0,24},{2,26},{4,28},{6,30},{8,16},{10,18},{12,20},{14,22},{16,8},... | collective-permute-start | bytes 196616 | tf_op jit(solution)/shard_map/ppermute | solution.py:109
  56.4 0.0 collective-permute-start.7
  56.4 2.1 %collective-permute-start.6 = (bf16[256,128]{1,0:T(8,128)(2,1)}, bf16[256,128]{1,0:T(8,128)(2,1)S(1)}, u32[]{:S(2)}, u32[]{:S(2)}) collective-permute-start(bf16[256,128]{1,0:T(8,128)(2,1)} %get-tuple-element.10), channel_id=1, source_target_pairs={{0,8},{2,10},{4,12},{6,14},{8,0},{10,2},{12,4},{14,6},{16,24},{18,... | collective-permute-start | bytes 196616 | tf_op jit(solution)/shard_map/ppermute | solution.py:109
  58.5 2.0 %collective-permute-done.8 = bf16[256,128]{1,0:T(8,128)(2,1)S(1)} collective-permute-done((bf16[256,128]{1,0:T(8,128)(2,1)}, bf16[256,128]{1,0:T(8,128)(2,1)S(1)}, u32[]{:S(2)}, u32[]{:S(2)}) %collective-permute-start.8) | collective-permute-done | bytes 65568 | tf_op jit(solution)/shard_map/ppermute | solution.py:109
  60.4 1.8 %collective-permute-done.7 = bf16[256,128]{1,0:T(8,128)(2,1)S(1)} collective-permute-done((bf16[256,128]{1,0:T(8,128)(2,1)}, bf16[256,128]{1,0:T(8,128)(2,1)S(1)}, u32[]{:S(2)}, u32[]{:S(2)}) %collective-permute-start.7) | collective-permute-done | bytes 65568 | tf_op jit(solution)/shard_map/ppermute | solution.py:109
  62.2 0.0 collective-permute-done.6
  62.2 0.9 %pad_maximum_fusion.5 = bf16[4,256,128]{2,1,0:T(8,128)(2,1)S(1)} fusion(bf16[1,256,128]{2,1,0:T(8,128)(2,1)S(1)} %bitcast.27, bf16[1,256,128]{2,1,0:T(8,128)(2,1)S(1)} %bitcast.28, bf16[1,256,128]{2,1,0:T(8,128)(2,1)S(1)} %bitcast.29, bf16[1,256,128]{2,1,0:T(8,128)(2,1)} %bitcast.26), kind=kLoop, calls=%fused_computation.5 | loop fusion | flops 393216 | bytes 524288 | tf_op jit(solution)/shard_map/stack | solution.py:151
  63.1 0.7 %pad_maximum_fusion.6 = bf16[256,512]{1,0:T(8,128)(2,1)} fusion(bf16[256,128]{1,0:T(8,128)(2,1)S(1)} %get-tuple-element.14, bf16[256,128]{1,0:T(8,128)(2,1)S(1)} %get-tuple-element.15, bf16[256,128]{1,0:T(8,128)(2,1)S(1)} %get-tuple-element.16, bf16[256,128]{1,0:T(8,128)(2,1)S(1)} %get-tuple-element.13), kind=kLoop, calls=%fused_computation.6 | loop fusion | flops 1048576 | bytes 524288 | tf_op jit(solution)/shard_map/concatenate | solution.py:153
  (16 shorter events, 0.1 us)
Async XLA Ops:
  0.0 0.7 %copy-start.10 = (s32[1,2]{1,0:T(1,128)S(1)}, s32[1,2]{1,0:T(1,128)}, u32[]{:S(2)}) copy-start(s32[1,2]{1,0:T(1,128)} %param.8) | copy-start | bytes 28
  0.8 1.1 %copy-start.6 = (bf16[256,512]{1,0:T(8,128)(2,1)S(1)}, bf16[256,512]{1,0:T(8,128)(2,1)}, u32[]{:S(2)}) copy-start(bf16[256,512]{1,0:T(8,128)(2,1)} %param.5) | copy-start | bytes 786436
  0.8 1.2 %copy-start.7 = (bf16[256,512]{1,0:T(8,128)(2,1)S(1)}, bf16[256,512]{1,0:T(8,128)(2,1)}, u32[]{:S(2)}) copy-start(bf16[256,512]{1,0:T(8,128)(2,1)} %param.7) | copy-start | bytes 786436
  2.9 11.0 %collective-permute-start.2 = (bf16[784,128]{1,0:T(8,128)(2,1)S(1)}, bf16[784,128]{1,0:T(8,128)(2,1)S(1)}, u32[]{:S(2)}, u32[]{:S(2)}) collective-permute-start(bf16[784,128]{1,0:T(8,128)(2,1)S(1)} %get-tuple-element.29), channel_id=1, source_target_pairs={{0,24},{2,26},{4,28},{6,30},{8,16},{10,18},{12,20},{14,22},{16,8},... | collective-permute-start | bytes 602120 | tf_op jit(solution)/shard_map/ppermute | solution.py:109
  8.0 17.1 %collective-permute-start = (bf16[784,128]{1,0:T(8,128)(2,1)S(1)}, bf16[784,128]{1,0:T(8,128)(2,1)S(1)}, u32[]{:S(2)}, u32[]{:S(2)}) collective-permute-start(bf16[784,128]{1,0:T(8,128)(2,1)S(1)} %get-tuple-element.30), channel_id=1, source_target_pairs={{0,8},{2,10},{4,12},{6,14},{8,0},{10,2},{12,4},{14,6},{16,24},{18,... | collective-permute-start | bytes 602120 | tf_op jit(solution)/shard_map/ppermute | solution.py:109
  8.0 17.0 %collective-permute-start.1 = (bf16[784,128]{1,0:T(8,128)(2,1)S(1)}, bf16[784,128]{1,0:T(8,128)(2,1)S(1)}, u32[]{:S(2)}, u32[]{:S(2)}) collective-permute-start(bf16[784,128]{1,0:T(8,128)(2,1)S(1)} %get-tuple-element.31), channel_id=1, source_target_pairs={{0,16},{2,18},{4,20},{6,22},{8,24},{10,26},{12,28},{14,30},{16,0},... | collective-permute-start | bytes 602120 | tf_op jit(solution)/shard_map/ppermute | solution.py:109
  13.9 11.2 %copy-start = (bf16[784,128]{1,0:T(8,128)(2,1)}, bf16[784,128]{1,0:T(8,128)(2,1)S(1)}, u32[]{:S(2)}) copy-start(bf16[784,128]{1,0:T(8,128)(2,1)S(1)} %collective-permute-done.2.refs_3_) | copy-start | bytes 602116
  25.0 0.7 %copy-start.2 = (bf16[784,128]{1,0:T(8,128)(2,1)}, bf16[784,128]{1,0:T(8,128)(2,1)S(1)}, u32[]{:S(2)}) copy-start(bf16[784,128]{1,0:T(8,128)(2,1)S(1)} %collective-permute-done.1.refs_2_) | copy-start | bytes 602116
  25.0 0.7 %copy-start.1 = (bf16[784,128]{1,0:T(8,128)(2,1)}, bf16[784,128]{1,0:T(8,128)(2,1)S(1)}, u32[]{:S(2)}) copy-start(bf16[784,128]{1,0:T(8,128)(2,1)S(1)} %collective-permute-done.refs_1_) | copy-start | bytes 602116
  25.7 1.7 %copy-start.9 = (s32[4096]{0:T(1024)S(1)}, s32[4096]{0:T(1024)}, u32[]{:S(2)}) copy-start(s32[4096]{0:T(1024)} %param.9) | copy-start | bytes 49156
  25.8 13.4 %collective-permute-start.4 = (bf16[4,528,128]{2,1,0:T(8,128)(2,1)S(1)}, bf16[4,528,128]{2,1,0:T(8,128)(2,1)S(1)}, u32[]{:S(2)}, u32[]{:S(2)}) collective-permute-start(bf16[4,528,128]{2,1,0:T(8,128)(2,1)S(1)} %pad_maximum_fusion), channel_id=1, source_target_pairs={{0,4},{2,6},{4,0},{6,2},{8,12},{10,14},{12,8},{14,10},{16,20},{18,... | collective-permute-start | bytes 1622024 | tf_op jit(solution)/shard_map/ppermute | solution.py:109
  27.9 13.2 %collective-permute-start.3 = (bf16[4,528,128]{2,1,0:T(8,128)(2,1)S(1)}, bf16[4,528,128]{2,1,0:T(8,128)(2,1)S(1)}, u32[]{:S(2)}, u32[]{:S(2)}) collective-permute-start(bf16[4,528,128]{2,1,0:T(8,128)(2,1)S(1)} %pad_maximum_fusion), channel_id=1, source_target_pairs={{0,2},{2,0},{4,6},{6,4},{8,10},{10,8},{12,14},{14,12},{16,18},{18,... | collective-permute-start | bytes 1622024 | tf_op jit(solution)/shard_map/ppermute | solution.py:109
  39.2 1.9 %copy-start.3 = (bf16[4,528,128]{2,1,0:T(8,128)(2,1)}, bf16[4,528,128]{2,1,0:T(8,128)(2,1)S(1)}, u32[]{:S(2)}) copy-start(bf16[4,528,128]{2,1,0:T(8,128)(2,1)S(1)} %collective-permute-done.4.refs_5_) | copy-start | bytes 1622020
  39.2 1.9 %collective-permute-start.5 = (bf16[4,528,128]{2,1,0:T(8,128)(2,1)S(1)}, bf16[4,528,128]{2,1,0:T(8,128)(2,1)S(1)}, u32[]{:S(2)}, u32[]{:S(2)}) collective-permute-start(bf16[4,528,128]{2,1,0:T(8,128)(2,1)S(1)} %collective-permute-done.4.refs_5_), channel_id=1, source_target_pairs={{0,2},{2,0},{4,6},{6,4},{8,10},{10,8},{12,14},{14,12},{16,18},{18,... | collective-permute-start | bytes 1622024 | tf_op jit(solution)/shard_map/ppermute | solution.py:109
  40.4 0.7 %copy-start.8 = (s32[32,128]{1,0:T(8,128)}, s32[32,128]{1,0:T(8,128)S(1)}, u32[]{:S(2)}) copy-start(s32[32,128]{1,0:T(8,128)S(1)} %broadcast_maximum_fusion.start_ref) | copy-start | bytes 49156
  41.1 0.8 %copy-start.4 = (bf16[4,528,128]{2,1,0:T(8,128)(2,1)}, bf16[4,528,128]{2,1,0:T(8,128)(2,1)S(1)}, u32[]{:S(2)}) copy-start(bf16[4,528,128]{2,1,0:T(8,128)(2,1)S(1)} %collective-permute-done.3.refs_4_) | copy-start | bytes 1622020
  41.1 1.0 %copy-start.5 = (bf16[4,528,128]{2,1,0:T(8,128)(2,1)}, bf16[4,528,128]{2,1,0:T(8,128)(2,1)S(1)}, u32[]{:S(2)}) copy-start(bf16[4,528,128]{2,1,0:T(8,128)(2,1)S(1)} %collective-permute-done.5.refs_6_) | copy-start | bytes 1622020
  54.1 6.3 %collective-permute-start.8 = (bf16[256,128]{1,0:T(8,128)(2,1)}, bf16[256,128]{1,0:T(8,128)(2,1)S(1)}, u32[]{:S(2)}, u32[]{:S(2)}) collective-permute-start(bf16[256,128]{1,0:T(8,128)(2,1)} %get-tuple-element.12), channel_id=1, source_target_pairs={{0,24},{2,26},{4,28},{6,30},{8,16},{10,18},{12,20},{14,22},{16,8},... | collective-permute-start | bytes 196616 | tf_op jit(solution)/shard_map/ppermute | solution.py:109
  56.4 5.8 %collective-permute-start.7 = (bf16[256,128]{1,0:T(8,128)(2,1)}, bf16[256,128]{1,0:T(8,128)(2,1)S(1)}, u32[]{:S(2)}, u32[]{:S(2)}) collective-permute-start(bf16[256,128]{1,0:T(8,128)(2,1)} %get-tuple-element.11), channel_id=1, source_target_pairs={{0,16},{2,18},{4,20},{6,22},{8,24},{10,26},{12,28},{14,30},{16,0},... | collective-permute-start | bytes 196616 | tf_op jit(solution)/shard_map/ppermute | solution.py:109
  56.4 5.8 %collective-permute-start.6 = (bf16[256,128]{1,0:T(8,128)(2,1)}, bf16[256,128]{1,0:T(8,128)(2,1)S(1)}, u32[]{:S(2)}, u32[]{:S(2)}) collective-permute-start(bf16[256,128]{1,0:T(8,128)(2,1)} %get-tuple-element.10), channel_id=1, source_target_pairs={{0,8},{2,10},{4,12},{6,14},{8,0},{10,2},{12,4},{14,6},{16,24},{18,... | collective-permute-start | bytes 196616 | tf_op jit(solution)/shard_map/ppermute | solution.py:109

commit v3 on v2

v3 whole, which is shorter than its diff:
```python
import functools
import math

import jax
import jax.numpy as jnp
from jax import lax
from jax.experimental import pallas as pl
from jax.experimental.pallas import tpu as pltpu
from jax.sharding import PartitionSpec as P

HEAD_DIM = 128
CHUNK = 512
HIDDEN = -1e30
NOTE_ROWS = 16
PAIR = 4


def attend_kernel(n_hi, n_lo, group, first_ref, start_ref, *refs):
    tok_rows = 2 * group
    piece_refs = refs[:n_hi]
    n_held = 2 * (n_lo - 1)
    held_refs = refs[n_hi:n_hi + n_held]
    out_refs = refs[n_hi + n_held:2 * n_hi + n_held]
    key_buf, value_buf, score_buf = refs[2 * n_hi + n_held:]
    half = 2
    factor = math.log2(math.e) / math.sqrt(HEAD_DIM)

    def stored(hi, lo, first, count):
        rows = slice(first, first + count)
        if lo == 0:
            return piece_refs[hi][rows]
        return held_refs[hi // half * (n_lo - 1) + lo - 1][hi % half, rows]

    def group_numbers(hi, lo):
        notes = stored(hi, lo, 2 * tok_rows, NOTE_ROWS).astype(jnp.float32).astype(jnp.int32)
        return notes[0, 0], notes[NOTE_ROWS // 2, 0]

    key_buf[:CHUNK] = jnp.zeros((CHUNK, HEAD_DIM), key_buf.dtype)
    value_buf[:CHUNK] = jnp.zeros((CHUNK, HEAD_DIM), value_buf.dtype)
    mine = []
    for lo in range(n_lo):
        for hi in range(n_hi):
            numbers = group_numbers(hi, lo)
            if lo == 0:
                mine.append(numbers)
            for slot in range(2):
                at = pl.multiple_of(numbers[slot] * group + CHUNK, group)
                key_buf[pl.ds(at, group)] = stored(hi, lo, slot * group, group)
                value_buf[pl.ds(at, group)] = stored(hi, lo, tok_rows + slot * group, group)

    lane = lax.broadcasted_iota(jnp.int32, (group, CHUNK), 1)
    row = lax.broadcasted_iota(jnp.int32, (group, CHUNK), 0)
    lanes = CHUNK // HEAD_DIM

    def by_lane(op, x):
        total = x[:, :HEAD_DIM]
        for i in range(1, lanes):
            total = op(total, x[:, i * HEAD_DIM:(i + 1) * HEAD_DIM])
        return total

    def attend(tasks):
        ends, lows, highs, queries = [], [], [], []
        count = 0
        for hi, slot in tasks:
            number = mine[hi][slot]
            end = (number + 1) * group
            count = jnp.maximum(count, (end - first_ref[number] + CHUNK - 1) // CHUNK)
            q_row = 2 * tok_rows + NOTE_ROWS + slot * group
            starts = jnp.broadcast_to(start_ref[pl.ds(number, 1), :], (group, group)).T[:, :1]
            ends.append(end)
            lows.append(starts - lane)
            highs.append(row - lane + (end - group))
            queries.append(piece_refs[hi][q_row:q_row + group, :])
        n = len(tasks)

        def rows_at(i, t):
            base = ends[t] - (i + 1) * CHUNK
            return base, pl.multiple_of(jnp.maximum(base + CHUNK, 0), group)

        def score(i, tops):
            out = []
            for t in range(n):
                base, at = rows_at(i, t)
                s = lax.dot_general(
                    queries[t], key_buf[pl.ds(at, CHUNK)],
                    (((1,), (1,)), ((), ())), preferred_element_type=jnp.float32,
                )
                s = jnp.where((lows[t] <= base) & (highs[t] >= base), s, HIDDEN)
                score_buf[t, i] = s
                out.append(jnp.maximum(tops[t], by_lane(jnp.maximum, s)))
            return tuple(out)

        hidden = jnp.full((group, HEAD_DIM), HIDDEN, jnp.float32)
        tops = lax.fori_loop(0, count, score, (hidden,) * n)
        tops = [jnp.max(top, axis=1, keepdims=True) for top in tops]

        def weigh(i, state):
            out = []
            for t in range(n):
                total, summed = state[t]
                _, at = rows_at(i, t)
                w = jnp.exp2((score_buf[t, i] - tops[t]) * factor)
                total = total + by_lane(jnp.add, w)
                summed = summed + jnp.dot(
                    w.astype(jnp.bfloat16), value_buf[pl.ds(at, CHUNK)],
                    preferred_element_type=jnp.float32,
                )
                out.append((total, summed))
            return tuple(out)

        zeros = jnp.zeros((group, HEAD_DIM), jnp.float32)
        state = lax.fori_loop(0, count, weigh, ((zeros, zeros),) * n)
        for (hi, slot), (total, summed) in zip(tasks, state):
            total = jnp.sum(total, axis=1, keepdims=True)
            rows = slice(slot * group, (slot + 1) * group)
            out_refs[hi][rows, :] = (summed / total).astype(jnp.bfloat16)

    for slot in range(2):
        for hi in range(0, n_hi, PAIR):
            attend([(hi + t, slot) for t in range(PAIR)])


def shards(n_blk, queries, keys, values, group_table, doc_ids):
    tok_rows = queries.shape[0]
    group = tok_rows // 2
    n_hi = queries.shape[1] // HEAD_DIM
    n_lo = n_blk // n_hi
    seq = doc_ids.shape[0]
    assert seq // group <= 256
    me = lax.axis_index("blk")
    my_hi = me // n_lo

    def swap(x, by):
        return lax.ppermute(x, "blk", [(b, b ^ by) for b in range(n_blk)])

    def head_of(x, hi):
        return lax.dynamic_slice(x, (0, hi * HEAD_DIM), (tok_rows, HEAD_DIM))

    notes = jnp.repeat(group_table[0], NOTE_ROWS // 2).astype(jnp.bfloat16)
    notes = jnp.broadcast_to(notes[:, None], (NOTE_ROWS, HEAD_DIM))
    kv_rows = 2 * tok_rows + NOTE_ROWS
    sends = []
    for step in range(n_hi):
        hi = my_hi ^ step
        sends.append(jnp.concatenate([head_of(keys, hi), head_of(values, hi), notes, head_of(queries, hi)]))
    first = n_lo // 2
    pieces = [swap(sends[step], step * n_lo) if step else sends[0] for step in range(n_hi)]
    across = [swap(sends[step][:kv_rows], step * n_lo + first) for step in range(2)]

    def gather(held, bit):
        while bit:
            for j in list(held):
                held[j ^ bit] = swap(held[j], bit)
            bit //= 2
        return [held[j] for j in range(1, n_lo)]

    near = jnp.stack([piece[:kv_rows] for piece in pieces[:2]])
    far = jnp.stack([piece[:kv_rows] for piece in pieces[2:]])
    batches = gather({0: near, first: jnp.stack(across)}, first // 2) + gather({0: far}, first)

    index = jnp.arange(seq, dtype=jnp.int32)
    before = jnp.concatenate([doc_ids[:1], doc_ids[:-1]])
    start = lax.cummax(jnp.where(doc_ids != before, index, 0))
    start = start.reshape(seq // group, group)

    smem = pl.BlockSpec(memory_space=pltpu.SMEM)
    vmem = pl.BlockSpec(memory_space=pltpu.VMEM)
    outs = pl.pallas_call(
        functools.partial(attend_kernel, n_hi, n_lo, group),
        out_shape=[jax.ShapeDtypeStruct((tok_rows, HEAD_DIM), jnp.bfloat16)] * n_hi,
        in_specs=[smem] + [vmem] * (1 + n_hi + 2 * (n_lo - 1)),
        out_specs=[vmem] * n_hi,
        scratch_shapes=[
            pltpu.VMEM((seq + CHUNK, HEAD_DIM), jnp.bfloat16),
            pltpu.VMEM((seq + CHUNK, HEAD_DIM), jnp.bfloat16),
            pltpu.VMEM((PAIR, seq // CHUNK, group, CHUNK), jnp.float32),
        ],
        name="attend",
    )(
        start[:, 0], start, *pieces, *batches,
    )
    back = jnp.stack([swap(outs[j], j * n_lo) if j else outs[0] for j in range(n_hi)])
    heads = [lax.dynamic_index_in_dim(back, my_hi ^ h, 0, keepdims=False) for h in range(n_hi)]
    return jnp.concatenate(heads, axis=1)


def solution(mesh):
    in_specs = (P("blk", "head"), P("blk", "head"), P("blk", "head"), P("blk", None), P())
    out_specs = P("blk", "head")
    body = functools.partial(shards, mesh.shape["blk"])
    return jax.shard_map(body, mesh=mesh, in_specs=in_specs, out_specs=out_specs, check_vma=False)
```

time: 64.3 us -> 57.6 us (0.90)
  waiting for transfers between devices: 31.6 us -> 24.5 us
  starting transfers between devices: 11.6 us -> 15.5 us
  Pallas kernels: 12 us -> 8.27 us
    ppermute x9 -> x13, waiting for transfers between devices: 31.6 us -> 24.5 us  [swap(): return lax.ppermute(x, 'blk', [(b, b ^ by) for b in range(n_blk)])]
    ppermute x9 -> x13, starting transfers between devices: 11.6 us -> 15.5 us  [swap(): return lax.ppermute(x, 'blk', [(b, b ^ by) for b in range(n_blk)])]
    pallas_call x1, Pallas kernels: 12 us -> 8.27 us  [shards(): pl.pallas_call(functools.partial(attend_kernel, n_hi, n_lo, group), out_s...]
    unnamed x22 -> x28, local copies, waits for them, and re-layouts: 2.39 us -> 2.75 us
  transfers between devices with their start and end apart: 9 -> 13, of which waited for: 6 -> 7; matrix products, arithmetic and copies ran while one was open for 4% -> 6% of each run, Pallas kernels for 0% -> 0%
where the time goes in v3:
time: 57.6 us; the launch traced here: 57.5 us
  waiting for transfers between devices  24.5 us (43%)
  starting transfers between devices  15.5 us (27%)
  Pallas kernels  8.27 us (14%)
  local copies, waits for them, and re-layouts  5.49 us (10%)
  other arithmetic  3.58 us (6%)
    ppermute x13, waiting for transfers between devices, swap(): return lax.ppermute(x, 'blk', [(b, b ^ by) for b in range(n_blk)])  24.5 us
    ppermute x13, starting transfers between devices, swap(): return lax.ppermute(x, 'blk', [(b, b ^ by) for b in range(n_blk)])  15.5 us
    pallas_call x1, Pallas kernels, shards(): pl.pallas_call(functools.partial(attend_kernel, n_hi, n_lo, group), out_s...  8.27 us
    unnamed x28, local copies, waits for them, and re-layouts  2.75 us
  transfers between devices with their start and end apart: 13, of which 7 were waited for; matrix products, arithmetic and copies ran while one was open for 6% of the time, Pallas kernels for 0%

profile of v3, /device:TPU:0, one launch (start us, length us, event | category | flops | bytes accessed | tf_op | source)
XLA Modules:
  0.0 57.5 jit_solution(1512187149633428808)
XLA Ops:
  0.0 0.7 %copy-done.13 = s32[1,2]{1,0:T(1,128)S(1)} copy-done((s32[1,2]{1,0:T(1,128)S(1)}, s32[1,2]{1,0:T(1,128)}, u32[]{:S(2)}) %copy-start.13) | copy-done | bytes 32
  0.7 0.1 broadcast_in_dim.14
  0.7 0.1 convert_element_type.16
  0.8 1.0 %constant_dynamic-slice_fusion.2 = (bf16[256,128]{1,0:T(8,128)(2,1)S(1)}, bf16[256,128]{1,0:T(8,128)(2,1)S(1)}, bf16[256,128]{1,0:T(8,128)(2,1)S(1)}, bf16[256,128]{1,0:T(8,128)(2,1)S(1)}) fusion(bf16[256,512]{1,0:T(8,128)(2,1)} %param.6, s32[]{:T(128)S(6)} %select_n.47, s32[]{:T(128)S(6)} %select_n.45, s32[]{:T(128)S(6)} %select_n.44, s32[]{:T(128)S(6)} %select_n.46), kind=kLoop, calls=%fused_computation.29 | loop fusion | bytes 524304 | tf_op jit(solution)/shard_map/dynamic_slice | solution.py:137
  1.8 0.1 copy-done.9
  1.9 0.1 copy-done.10
  2.0 0.1 constant_dynamic-slice_fusion
  2.1 0.1 broadcast_in_dim.15
  2.2 3.1 %collective-permute-start.4 = (bf16[528,128]{1,0:T(8,128)(2,1)S(1)}, bf16[528,128]{1,0:T(8,128)(2,1)S(1)}, u32[]{:S(2)}, u32[]{:S(2)}) collective-permute-start(bf16[528,128]{1,0:T(8,128)(2,1)S(1)} %get-tuple-element.29), channel_id=1, source_target_pairs={{0,4},{2,6},{4,0},{6,2},{8,12},{10,14},{12,8},{14,10},{16,20},{18,... | collective-permute-start | bytes 405512 | tf_op jit(solution)/shard_map/ppermute | solution.py:134
  5.3 1.5 %collective-permute-start.5 = (bf16[528,128]{1,0:T(8,128)(2,1)S(1)}, bf16[528,128]{1,0:T(8,128)(2,1)S(1)}, u32[]{:S(2)}, u32[]{:S(2)}) collective-permute-start(bf16[528,128]{1,0:T(8,128)(2,1)S(1)} %get-tuple-element.31), channel_id=1, source_target_pairs={{0,12},{2,14},{4,8},{6,10},{8,4},{10,6},{12,0},{14,2},{16,28},{18,... | collective-permute-start | bytes 405512 | tf_op jit(solution)/shard_map/ppermute | solution.py:134
  6.8 0.7 %fusion.3 = (bf16[784,128]{1,0:T(8,128)(2,1)S(1)}, bf16[784,128]{1,0:T(8,128)(2,1)S(1)}, bf16[784,128]{1,0:T(8,128)(2,1)S(1)}, bf16[784,128]{1,0:T(8,128)(2,1)}) fusion(bf16[16,128]{1,0:T(8,128)(2,1)S(1)} %broadcast_in_dim.15, bf16[256,128]{1,0:T(8,128)(2,1)S(1)} %get-tuple-element.25, bf16[256,128]{1,0:T(8,128)(2,1)S(1)} %get-tuple-element.39, ...), kind=kLoop, calls=%fused_computation.12 | loop fusion | flops 2910208 | bytes 1593344 | tf_op jit(solution)/shard_map/concatenate | solution.py:145
  7.5 2.5 %collective-permute-start.2 = (bf16[784,128]{1,0:T(8,128)(2,1)S(1)}, bf16[784,128]{1,0:T(8,128)(2,1)S(1)}, u32[]{:S(2)}, u32[]{:S(2)}) collective-permute-start(bf16[784,128]{1,0:T(8,128)(2,1)S(1)} %get-tuple-element.32), channel_id=1, source_target_pairs={{0,24},{2,26},{4,28},{6,30},{8,16},{10,18},{12,20},{14,22},{16,8},... | collective-permute-start | bytes 602120 | tf_op jit(solution)/shard_map/ppermute | solution.py:134
  10.0 0.7 %collective-permute-start = (bf16[784,128]{1,0:T(8,128)(2,1)S(1)}, bf16[784,128]{1,0:T(8,128)(2,1)S(1)}, u32[]{:S(2)}, u32[]{:S(2)}) collective-permute-start(bf16[784,128]{1,0:T(8,128)(2,1)S(1)} %get-tuple-element.33), channel_id=1, source_target_pairs={{0,8},{2,10},{4,12},{6,14},{8,0},{10,2},{12,4},{14,6},{16,24},{18,... | collective-permute-start | bytes 602120 | tf_op jit(solution)/shard_map/ppermute | solution.py:134
  10.7 1.2 %collective-permute-start.1 = (bf16[784,128]{1,0:T(8,128)(2,1)S(1)}, bf16[784,128]{1,0:T(8,128)(2,1)S(1)}, u32[]{:S(2)}, u32[]{:S(2)}) collective-permute-start(bf16[784,128]{1,0:T(8,128)(2,1)S(1)} %get-tuple-element.34), channel_id=1, source_target_pairs={{0,16},{2,18},{4,20},{6,22},{8,24},{10,26},{12,28},{14,30},{16,0},... | collective-permute-start | bytes 602120 | tf_op jit(solution)/shard_map/ppermute | solution.py:134
  11.9 0.5 slice.30
  12.4 0.7 %select_bitcast_fusion = s32[32,128]{1,0:T(8,128)S(1)} fusion(s32[4096]{0:T(1024)S(1)} %copy-done.12, s32[4095]{0:T(1024)S(1)} %bitcast.29, s32[1]{0:T(128)} %slice.30), kind=kLoop, calls=%fused_computation.25 | loop fusion | flops 12288 | bytes 49152 | tf_op jit(solution)/shard_map/reshape
  13.1 0.3 reduce-window.9
  13.4 0.1 slice.38
  13.5 0.1 reduce-window.12
  13.6 0.1 slice_reduce_fusion.1
  13.7 0.0 collective-permute-done.4
  13.7 0.0 collective-permute-done.5
  13.7 0.1 collective-permute-start.6
  13.8 4.0 %collective-permute-done.2.refs_3_ = bf16[784,128]{1,0:T(8,128)(2,1)S(1)} collective-permute-done((bf16[784,128]{1,0:T(8,128)(2,1)S(1)}, bf16[784,128]{1,0:T(8,128)(2,1)S(1)}, u32[]{:S(2)}, u32[]{:S(2)}) %collective-permute-start.2) | collective-permute-done | bytes 200736 | tf_op jit(solution)/shard_map/ppermute | solution.py:134
  17.8 9.6 %collective-permute-done.1.refs_2_ = bf16[784,128]{1,0:T(8,128)(2,1)S(1)} collective-permute-done((bf16[784,128]{1,0:T(8,128)(2,1)S(1)}, bf16[784,128]{1,0:T(8,128)(2,1)S(1)}, u32[]{:S(2)}, u32[]{:S(2)}) %collective-permute-start.1) | collective-permute-done | bytes 200736 | tf_op jit(solution)/shard_map/ppermute | solution.py:134
  27.5 0.6 %copy-done.3 = bf16[784,128]{1,0:T(8,128)(2,1)} copy-done((bf16[784,128]{1,0:T(8,128)(2,1)}, bf16[784,128]{1,0:T(8,128)(2,1)S(1)}, u32[]{:S(2)}) %copy-start.3) | copy-done | bytes 200728
  28.1 1.5 %collective-permute-start.8 = (bf16[2,528,128]{2,1,0:T(8,128)(2,1)S(1)}, bf16[2,528,128]{2,1,0:T(8,128)(2,1)S(1)}, u32[]{:S(2)}, u32[]{:S(2)}) collective-permute-start(bf16[2,528,128]{2,1,0:T(8,128)(2,1)S(1)} %pad_maximum_fusion.6), channel_id=1, source_target_pairs={{0,4},{2,6},{4,0},{6,2},{8,12},{10,14},{12,8},{14,10},{16,20},{18,... | collective-permute-start | bytes 811016 | tf_op jit(solution)/shard_map/ppermute | solution.py:134
  29.6 0.0 collective-permute-start.7
  29.6 0.0 collective-permute-done.refs_1_
  29.7 0.6 %copy-done.2 = bf16[784,128]{1,0:T(8,128)(2,1)} copy-done((bf16[784,128]{1,0:T(8,128)(2,1)}, bf16[784,128]{1,0:T(8,128)(2,1)S(1)}, u32[]{:S(2)}) %copy-start.2) | copy-done | bytes 200728
  30.3 0.5 collective-permute-start.3
  30.8 4.6 %collective-permute-done.8.refs_8_ = bf16[2,528,128]{2,1,0:T(8,128)(2,1)S(1)} collective-permute-done((bf16[2,528,128]{2,1,0:T(8,128)(2,1)S(1)}, bf16[2,528,128]{2,1,0:T(8,128)(2,1)S(1)}, u32[]{:S(2)}, u32[]{:S(2)}) %collective-permute-start.8) | collective-permute-done | bytes 270368 | tf_op jit(solution)/shard_map/ppermute | solution.py:134
  35.4 0.1 broadcast_maximum_fusion.start_ref
  35.5 0.6 %slice_reduce_fusion.first_ref = s32[32]{0:T(128)} fusion(s32[32,128]{1,0:T(8,128)S(1)} %broadcast_maximum_fusion.start_ref), kind=kLoop, calls=%fused_computation.22 | loop fusion | bytes 256 | tf_op jit(solution)/shard_map/slice | solution.py:180
  36.1 0.0 collective-permute-done.6.refs_6_
  36.1 0.0 collective-permute-done.7.refs_7_
  36.2 0.8 %collective-permute-done.9.refs_9_ = bf16[2,528,128]{2,1,0:T(8,128)(2,1)S(1)} collective-permute-done((bf16[2,528,128]{2,1,0:T(8,128)(2,1)S(1)}, bf16[2,528,128]{2,1,0:T(8,128)(2,1)S(1)}, u32[]{:S(2)}, u32[]{:S(2)}) %collective-permute-start.9) | collective-permute-done | bytes 270368 | tf_op jit(solution)/shard_map/ppermute | solution.py:134
  37.0 0.0 copy-done.7
  37.0 0.7 %copy-done.8 = bf16[2,528,128]{2,1,0:T(8,128)(2,1)} copy-done((bf16[2,528,128]{2,1,0:T(8,128)(2,1)}, bf16[2,528,128]{2,1,0:T(8,128)(2,1)S(1)}, u32[]{:S(2)}) %copy-start.8) | copy-done | bytes 270360
  37.7 8.3 %attend.1 = (bf16[256,128]{1,0:T(8,128)(2,1)}, bf16[256,128]{1,0:T(8,128)(2,1)}, bf16[256,128]{1,0:T(8,128)(2,1)}, bf16[256,128]{1,0:T(8,128)(2,1)}) custom-call(s32[32]{0:T(128)} %slice_reduce_fusion.first_ref, s32[32,128]{1,0:T(8,128)} %copy-done.11, bf16[784,128]{1,0:T(8,128)(2,1)} %get-tuple-element.35.refs_0_, bf16[784,128]{1,0:T(8,128)(2,1)} %copy-done.2, ...), custom_call_target="tpu_custom_call" | custom-call | tf_op jit(solution)/shard_map/attend/pallas_call | solution.py:168
  46.0 0.1 collective-permute-start.10
  46.1 3.4 %collective-permute-start.11 = (bf16[256,128]{1,0:T(8,128)(2,1)}, bf16[256,128]{1,0:T(8,128)(2,1)S(1)}, u32[]{:S(2)}, u32[]{:S(2)}) collective-permute-start(bf16[256,128]{1,0:T(8,128)(2,1)} %get-tuple-element.11), channel_id=1, source_target_pairs={{0,16},{2,18},{4,20},{6,22},{8,24},{10,26},{12,28},{14,30},{16,0},... | collective-permute-start | bytes 196616 | tf_op jit(solution)/shard_map/ppermute | solution.py:134
  49.5 0.9 %collective-permute-start.12 = (bf16[256,128]{1,0:T(8,128)(2,1)}, bf16[256,128]{1,0:T(8,128)(2,1)S(1)}, u32[]{:S(2)}, u32[]{:S(2)}) collective-permute-start(bf16[256,128]{1,0:T(8,128)(2,1)} %get-tuple-element.12), channel_id=1, source_target_pairs={{0,24},{2,26},{4,28},{6,30},{8,16},{10,18},{12,20},{14,22},{16,8},... | collective-permute-start | bytes 196616 | tf_op jit(solution)/shard_map/ppermute | solution.py:134
  50.3 0.1 collective-permute-done.10
  50.4 3.3 %collective-permute-done.11 = bf16[256,128]{1,0:T(8,128)(2,1)S(1)} collective-permute-done((bf16[256,128]{1,0:T(8,128)(2,1)}, bf16[256,128]{1,0:T(8,128)(2,1)S(1)}, u32[]{:S(2)}, u32[]{:S(2)}) %collective-permute-start.11) | collective-permute-done | bytes 65568 | tf_op jit(solution)/shard_map/ppermute | solution.py:134
  53.7 2.1 %collective-permute-done.12 = bf16[256,128]{1,0:T(8,128)(2,1)S(1)} collective-permute-done((bf16[256,128]{1,0:T(8,128)(2,1)}, bf16[256,128]{1,0:T(8,128)(2,1)S(1)}, u32[]{:S(2)}, u32[]{:S(2)}) %collective-permute-start.12) | collective-permute-done | bytes 65568 | tf_op jit(solution)/shard_map/ppermute | solution.py:134
  55.8 0.9 %pad_maximum_fusion.7 = bf16[4,256,128]{2,1,0:T(8,128)(2,1)S(1)} fusion(bf16[1,256,128]{2,1,0:T(8,128)(2,1)S(1)} %bitcast.33, bf16[1,256,128]{2,1,0:T(8,128)(2,1)S(1)} %bitcast.32, bf16[1,256,128]{2,1,0:T(8,128)(2,1)S(1)} %bitcast.31, bf16[1,256,128]{2,1,0:T(8,128)(2,1)} %bitcast.30), kind=kLoop, calls=%fused_computation.7 | loop fusion | flops 393216 | bytes 524288 | tf_op jit(solution)/shard_map/stack | solution.py:182
  56.7 0.7 %pad_maximum_fusion.8 = bf16[256,512]{1,0:T(8,128)(2,1)} fusion(bf16[256,128]{1,0:T(8,128)(2,1)S(1)} %get-tuple-element.14, bf16[256,128]{1,0:T(8,128)(2,1)S(1)} %get-tuple-element.15, bf16[256,128]{1,0:T(8,128)(2,1)S(1)} %get-tuple-element.16, bf16[256,128]{1,0:T(8,128)(2,1)S(1)} %get-tuple-element.13), kind=kLoop, calls=%fused_computation.8 | loop fusion | flops 1048576 | bytes 524288 | tf_op jit(solution)/shard_map/concatenate | solution.py:184
  (32 shorter events, 0.2 us)
Async XLA Ops:
  0.0 0.7 %copy-start.13 = (s32[1,2]{1,0:T(1,128)S(1)}, s32[1,2]{1,0:T(1,128)}, u32[]{:S(2)}) copy-start(s32[1,2]{1,0:T(1,128)} %param.8) | copy-start | bytes 28
  0.8 1.1 %copy-start.9 = (bf16[256,512]{1,0:T(8,128)(2,1)S(1)}, bf16[256,512]{1,0:T(8,128)(2,1)}, u32[]{:S(2)}) copy-start(bf16[256,512]{1,0:T(8,128)(2,1)} %param.5) | copy-start | bytes 786436
  0.8 1.2 %copy-start.10 = (bf16[256,512]{1,0:T(8,128)(2,1)S(1)}, bf16[256,512]{1,0:T(8,128)(2,1)}, u32[]{:S(2)}) copy-start(bf16[256,512]{1,0:T(8,128)(2,1)} %param.7) | copy-start | bytes 786436
  2.2 11.5 %collective-permute-start.4 = (bf16[528,128]{1,0:T(8,128)(2,1)S(1)}, bf16[528,128]{1,0:T(8,128)(2,1)S(1)}, u32[]{:S(2)}, u32[]{:S(2)}) collective-permute-start(bf16[528,128]{1,0:T(8,128)(2,1)S(1)} %get-tuple-element.29), channel_id=1, source_target_pairs={{0,4},{2,6},{4,0},{6,2},{8,12},{10,14},{12,8},{14,10},{16,20},{18,... | collective-permute-start | bytes 405512 | tf_op jit(solution)/shard_map/ppermute | solution.py:134
  5.3 8.4 %collective-permute-start.5 = (bf16[528,128]{1,0:T(8,128)(2,1)S(1)}, bf16[528,128]{1,0:T(8,128)(2,1)S(1)}, u32[]{:S(2)}, u32[]{:S(2)}) collective-permute-start(bf16[528,128]{1,0:T(8,128)(2,1)S(1)} %get-tuple-element.31), channel_id=1, source_target_pairs={{0,12},{2,14},{4,8},{6,10},{8,4},{10,6},{12,0},{14,2},{16,28},{18,... | collective-permute-start | bytes 405512 | tf_op jit(solution)/shard_map/ppermute | solution.py:134
  6.8 5.1 %copy-start.12 = (s32[4096]{0:T(1024)S(1)}, s32[4096]{0:T(1024)}, u32[]{:S(2)}) copy-start(s32[4096]{0:T(1024)} %param.9) | copy-start | bytes 49156
  7.5 10.3 %collective-permute-start.2 = (bf16[784,128]{1,0:T(8,128)(2,1)S(1)}, bf16[784,128]{1,0:T(8,128)(2,1)S(1)}, u32[]{:S(2)}, u32[]{:S(2)}) collective-permute-start(bf16[784,128]{1,0:T(8,128)(2,1)S(1)} %get-tuple-element.32), channel_id=1, source_target_pairs={{0,24},{2,26},{4,28},{6,30},{8,16},{10,18},{12,20},{14,22},{16,8},... | collective-permute-start | bytes 602120 | tf_op jit(solution)/shard_map/ppermute | solution.py:134
  10.0 19.6 %collective-permute-start = (bf16[784,128]{1,0:T(8,128)(2,1)S(1)}, bf16[784,128]{1,0:T(8,128)(2,1)S(1)}, u32[]{:S(2)}, u32[]{:S(2)}) collective-permute-start(bf16[784,128]{1,0:T(8,128)(2,1)S(1)} %get-tuple-element.33), channel_id=1, source_target_pairs={{0,8},{2,10},{4,12},{6,14},{8,0},{10,2},{12,4},{14,6},{16,24},{18,... | collective-permute-start | bytes 602120 | tf_op jit(solution)/shard_map/ppermute | solution.py:134
  10.7 16.8 %collective-permute-start.1 = (bf16[784,128]{1,0:T(8,128)(2,1)S(1)}, bf16[784,128]{1,0:T(8,128)(2,1)S(1)}, u32[]{:S(2)}, u32[]{:S(2)}) collective-permute-start(bf16[784,128]{1,0:T(8,128)(2,1)S(1)} %get-tuple-element.34), channel_id=1, source_target_pairs={{0,16},{2,18},{4,20},{6,22},{8,24},{10,26},{12,28},{14,30},{16,0},... | collective-permute-start | bytes 602120 | tf_op jit(solution)/shard_map/ppermute | solution.py:134
  13.7 13.7 %copy-start = (bf16[2,528,128]{2,1,0:T(8,128)(2,1)}, bf16[2,528,128]{2,1,0:T(8,128)(2,1)S(1)}, u32[]{:S(2)}) copy-start(bf16[2,528,128]{2,1,0:T(8,128)(2,1)S(1)} %pad_maximum_fusion.5.refs_5_) | copy-start | bytes 811012
  13.7 22.4 %collective-permute-start.6 = (bf16[2,528,128]{2,1,0:T(8,128)(2,1)S(1)}, bf16[2,528,128]{2,1,0:T(8,128)(2,1)S(1)}, u32[]{:S(2)}, u32[]{:S(2)}) collective-permute-start(bf16[2,528,128]{2,1,0:T(8,128)(2,1)S(1)} %pad_maximum_fusion.5.refs_5_), channel_id=1, source_target_pairs={{0,2},{2,0},{4,6},{6,4},{8,10},{10,8},{12,14},{14,12},{16,18},{18,... | collective-permute-start | bytes 811016 | tf_op jit(solution)/shard_map/ppermute | solution.py:134
  17.8 9.7 %copy-start.1 = (bf16[784,128]{1,0:T(8,128)(2,1)}, bf16[784,128]{1,0:T(8,128)(2,1)S(1)}, u32[]{:S(2)}) copy-start(bf16[784,128]{1,0:T(8,128)(2,1)S(1)} %collective-permute-done.2.refs_3_) | copy-start | bytes 602116
  27.4 0.7 %copy-start.3 = (bf16[784,128]{1,0:T(8,128)(2,1)}, bf16[784,128]{1,0:T(8,128)(2,1)S(1)}, u32[]{:S(2)}) copy-start(bf16[784,128]{1,0:T(8,128)(2,1)S(1)} %collective-permute-done.1.refs_2_) | copy-start | bytes 602116
  28.1 7.3 %collective-permute-start.8 = (bf16[2,528,128]{2,1,0:T(8,128)(2,1)S(1)}, bf16[2,528,128]{2,1,0:T(8,128)(2,1)S(1)}, u32[]{:S(2)}, u32[]{:S(2)}) collective-permute-start(bf16[2,528,128]{2,1,0:T(8,128)(2,1)S(1)} %pad_maximum_fusion.6), channel_id=1, source_target_pairs={{0,4},{2,6},{4,0},{6,2},{8,12},{10,14},{12,8},{14,10},{16,20},{18,... | collective-permute-start | bytes 811016 | tf_op jit(solution)/shard_map/ppermute | solution.py:134
  29.6 6.5 %collective-permute-start.7 = (bf16[2,528,128]{2,1,0:T(8,128)(2,1)S(1)}, bf16[2,528,128]{2,1,0:T(8,128)(2,1)S(1)}, u32[]{:S(2)}, u32[]{:S(2)}) collective-permute-start(bf16[2,528,128]{2,1,0:T(8,128)(2,1)S(1)} %pad_maximum_fusion.6), channel_id=1, source_target_pairs={{0,2},{2,0},{4,6},{6,4},{8,10},{10,8},{12,14},{14,12},{16,18},{18,... | collective-permute-start | bytes 811016 | tf_op jit(solution)/shard_map/ppermute | solution.py:134
  29.6 0.7 %copy-start.2 = (bf16[784,128]{1,0:T(8,128)(2,1)}, bf16[784,128]{1,0:T(8,128)(2,1)S(1)}, u32[]{:S(2)}) copy-start(bf16[784,128]{1,0:T(8,128)(2,1)S(1)} %collective-permute-done.refs_1_) | copy-start | bytes 602116
  30.3 5.8 %collective-permute-start.3 = (bf16[2,528,128]{2,1,0:T(8,128)(2,1)S(1)}, bf16[2,528,128]{2,1,0:T(8,128)(2,1)S(1)}, u32[]{:S(2)}, u32[]{:S(2)}) collective-permute-start(bf16[2,528,128]{2,1,0:T(8,128)(2,1)S(1)} %pad_maximum_fusion.4), channel_id=1, source_target_pairs={{0,2},{2,0},{4,6},{6,4},{8,10},{10,8},{12,14},{14,12},{16,18},{18,... | collective-permute-start | bytes 811016 | tf_op jit(solution)/shard_map/ppermute | solution.py:134
  35.4 1.6 %copy-start.5 = (bf16[2,528,128]{2,1,0:T(8,128)(2,1)}, bf16[2,528,128]{2,1,0:T(8,128)(2,1)S(1)}, u32[]{:S(2)}) copy-start(bf16[2,528,128]{2,1,0:T(8,128)(2,1)S(1)} %collective-permute-done.8.refs_8_) | copy-start | bytes 811012
  35.4 1.5 %collective-permute-start.9 = (bf16[2,528,128]{2,1,0:T(8,128)(2,1)S(1)}, bf16[2,528,128]{2,1,0:T(8,128)(2,1)S(1)}, u32[]{:S(2)}, u32[]{:S(2)}) collective-permute-start(bf16[2,528,128]{2,1,0:T(8,128)(2,1)S(1)} %collective-permute-done.8.refs_8_), channel_id=1, source_target_pairs={{0,2},{2,0},{4,6},{6,4},{8,10},{10,8},{12,14},{14,12},{16,18},{18,... | collective-permute-start | bytes 811016 | tf_op jit(solution)/shard_map/ppermute | solution.py:134
  35.5 1.5 %copy-start.11 = (s32[32,128]{1,0:T(8,128)}, s32[32,128]{1,0:T(8,128)S(1)}, u32[]{:S(2)}) copy-start(s32[32,128]{1,0:T(8,128)S(1)} %broadcast_maximum_fusion.start_ref) | copy-start | bytes 49156
  36.1 0.9 %copy-start.4 = (bf16[2,528,128]{2,1,0:T(8,128)(2,1)}, bf16[2,528,128]{2,1,0:T(8,128)(2,1)S(1)}, u32[]{:S(2)}) copy-start(bf16[2,528,128]{2,1,0:T(8,128)(2,1)S(1)} %collective-permute-done.6.refs_6_) | copy-start | bytes 811012
  36.1 0.9 %copy-start.6 = (bf16[2,528,128]{2,1,0:T(8,128)(2,1)}, bf16[2,528,128]{2,1,0:T(8,128)(2,1)S(1)}, u32[]{:S(2)}) copy-start(bf16[2,528,128]{2,1,0:T(8,128)(2,1)S(1)} %collective-permute-done.7.refs_7_) | copy-start | bytes 811012
  36.2 0.9 %copy-start.7 = (bf16[2,528,128]{2,1,0:T(8,128)(2,1)}, bf16[2,528,128]{2,1,0:T(8,128)(2,1)S(1)}, u32[]{:S(2)}) copy-start(bf16[2,528,128]{2,1,0:T(8,128)(2,1)S(1)} %collective-permute-done.3.refs_4_) | copy-start | bytes 811012
  37.0 0.7 %copy-start.8 = (bf16[2,528,128]{2,1,0:T(8,128)(2,1)}, bf16[2,528,128]{2,1,0:T(8,128)(2,1)S(1)}, u32[]{:S(2)}) copy-start(bf16[2,528,128]{2,1,0:T(8,128)(2,1)S(1)} %collective-permute-done.9.refs_9_) | copy-start | bytes 811012
  46.0 4.5 %collective-permute-start.10 = (bf16[256,128]{1,0:T(8,128)(2,1)}, bf16[256,128]{1,0:T(8,128)(2,1)S(1)}, u32[]{:S(2)}, u32[]{:S(2)}) collective-permute-start(bf16[256,128]{1,0:T(8,128)(2,1)} %get-tuple-element.10), channel_id=1, source_target_pairs={{0,8},{2,10},{4,12},{6,14},{8,0},{10,2},{12,4},{14,6},{16,24},{18,... | collective-permute-start | bytes 196616 | tf_op jit(solution)/shard_map/ppermute | solution.py:134
  46.1 7.6 %collective-permute-start.11 = (bf16[256,128]{1,0:T(8,128)(2,1)}, bf16[256,128]{1,0:T(8,128)(2,1)S(1)}, u32[]{:S(2)}, u32[]{:S(2)}) collective-permute-start(bf16[256,128]{1,0:T(8,128)(2,1)} %get-tuple-element.11), channel_id=1, source_target_pairs={{0,16},{2,18},{4,20},{6,22},{8,24},{10,26},{12,28},{14,30},{16,0},... | collective-permute-start | bytes 196616 | tf_op jit(solution)/shard_map/ppermute | solution.py:134
  49.5 6.4 %collective-permute-start.12 = (bf16[256,128]{1,0:T(8,128)(2,1)}, bf16[256,128]{1,0:T(8,128)(2,1)S(1)}, u32[]{:S(2)}, u32[]{:S(2)}) collective-permute-start(bf16[256,128]{1,0:T(8,128)(2,1)} %get-tuple-element.12), channel_id=1, source_target_pairs={{0,24},{2,26},{4,28},{6,30},{8,16},{10,18},{12,20},{14,22},{16,8},... | collective-permute-start | bytes 196616 | tf_op jit(solution)/shard_map/ppermute | solution.py:134
